TPU v7x, 32 devices: a whole 2x2x4 slice. The times are simulated.
32 devices in a mesh: dp: 4 (over y, x), fsdp: 8 (over z, core).
Axes of the slice: x: 2, y: 2, z: 4, core: 2. Of those that a mesh axis runs over, the one named last changes fastest.
Arguments:
- hidden: bfloat16 [16384, 4096], P(('dp', 'fsdp')), may hold values from -6 to 6
- queries: bfloat16 [16384, 2048], P(('dp', 'fsdp')), may hold values from -60 to 60
- cotangent: bfloat16 [16384, 2048], P(('dp', 'fsdp')), may hold values from -0.125 to 0.125
- point_start: bfloat16 [4096, 1024], P('fsdp', 'dp'), may hold values from -0.09375 to 0.09375
- point_mid: bfloat16 [4096, 1024], P('fsdp', 'dp'), may hold values from -0.09375 to 0.09375
- point_end: bfloat16 [4096, 1024], P('fsdp', 'dp'), may hold values from -0.09375 to 0.09375
- curve_time: float32 [1], replicated, may hold values from 0.15 to 0.85
Outputs:
- context: bfloat16 [16384, 2048], P(('dp', 'fsdp'))
- gradient: float32 [4096, 1024], P('fsdp', 'dp')
All inputs are finite; a program needn't handle non-finite values.
Results may differ from a plain program's by a relative error of at most 0.0071.
Values may be sent and summed in bfloat16 or wider, within the bound.
A program may use at most 128 MiB of HBM per device.

v0:
```python
import functools
import math

import jax
import jax.numpy as jnp
from jax import lax
from jax.experimental import pallas as pl
from jax.experimental.pallas import tpu as pltpu
from jax.sharding import PartitionSpec as P

KVH = 4
HD = 128
BQ = 256
MESH = pl.DeviceIdType.MESH
VMEM_LIMIT = 60 * 1024 * 1024


def rope_tables(seq_len, head_dim):
    shape = (seq_len, head_dim)
    positions = lax.broadcasted_iota(jnp.int32, shape, 0).astype(jnp.float32)
    column = lax.broadcasted_iota(jnp.int32, shape, 1)
    halves_index = jnp.where(column < head_dim // 2, column, column - head_dim // 2).astype(jnp.float32)
    inverse = jnp.exp(-(2.0 * halves_index / head_dim) * math.log(500000.0))
    angles = positions * inverse
    cosine, sine_t = jnp.cos(angles), jnp.sin(angles)
    return (cosine, sine_t)


def rotate(x):
    half = x.shape[-1] // 2
    return jnp.concatenate([-x[..., half:], x[..., :half]], axis=-1)


def rotate_back(x):
    half = x.shape[-1] // 2
    return jnp.concatenate([x[..., half:], -x[..., :half]], axis=-1)


NN = (((1,), (0,)), ((), ()))
NT = (((1,), (1,)), ((), ()))
TN = (((0,), (0,)), ((), ()))


def mm(x, y, dims=NN):
    return lax.dot_general(x, y, dims, preferred_element_type=jnp.float32)


def attend_kernel(k_ref, v_ref, q_ref, g_ref, cos_ref, sin_ref, ctx_ref, grad_ref, kg, vg):
    seq = k_ref.shape[0]
    group = q_ref.shape[1] // HD
    scale = 1.0 / math.sqrt(HD)
    to_base2 = scale * math.log2(math.e)
    raw = k_ref[...].astype(jnp.float32)
    cosine, sine_t = cos_ref[...], sin_ref[...]
    keys = (raw * cosine + rotate(raw) * sine_t).astype(jnp.bfloat16)
    values = v_ref[...]
    values_t = values.astype(jnp.float32).T.astype(jnp.bfloat16)
    kg[...] = jnp.zeros_like(kg)
    vg[...] = jnp.zeros_like(vg)
    for start in range(0, seq, BQ):
        nk = start + BQ
        rows = slice(start, nk)
        qs = jnp.concatenate([q_ref[rows, g * HD:(g + 1) * HD] for g in range(group)], axis=0)
        gs = jnp.concatenate([g_ref[rows, g * HD:(g + 1) * HD] for g in range(group)], axis=0)
        s = mm(keys[:nk], qs, NT)
        key_at = lax.broadcasted_iota(jnp.int32, (BQ, group * BQ), 0)
        query_at = lax.broadcasted_iota(jnp.int32, (BQ, group * BQ), 1) % BQ
        last = jnp.where(key_at <= query_at, s[start:], -1e30)
        s = last if start == 0 else jnp.concatenate([s[:start], last], axis=0)
        top = jnp.max(s, axis=0, keepdims=True)
        w = jnp.exp2((s - top) * to_base2)
        p = w * (1.0 / jnp.sum(w, axis=0, keepdims=True))
        p_low = p.astype(jnp.bfloat16)
        ctx_t = mm(values_t[:, :nk], p_low)
        dp = mm(values[:nk], gs, NT)
        vg[:nk] += mm(p_low, gs)
        delta = jnp.sum(dp * p, axis=0, keepdims=True)
        ds = (p * ((dp - delta) * scale)).astype(jnp.bfloat16)
        kg[:nk] += mm(ds, qs)
        ctx = ctx_t.T.astype(jnp.bfloat16)
        for g in range(group):
            ctx_ref[rows, g * HD:(g + 1) * HD] = ctx[g * BQ:(g + 1) * BQ]
    rot = kg[...]
    grad_ref[0] = (rot * cosine + rotate_back(rot * sine_t)).astype(jnp.bfloat16)
    grad_ref[1] = vg[...].astype(jnp.bfloat16)


def attend(kv_rows, queries, cotangent, cosine, sine_t):
    seq = kv_rows.shape[0]
    heads = kv_rows.shape[1] // (2 * HD)
    width = queries.shape[1] // heads
    return pl.pallas_call(
        attend_kernel,
        grid=(heads,),
        out_shape=(
            jax.ShapeDtypeStruct(queries.shape, jnp.bfloat16),
            jax.ShapeDtypeStruct((2, seq, heads * HD), jnp.bfloat16),
        ),
        in_specs=[
            pl.BlockSpec((seq, HD), lambda j: (0, j)),
            pl.BlockSpec((seq, HD), lambda j: (0, j + heads)),
            pl.BlockSpec((seq, width), lambda j: (0, j)),
            pl.BlockSpec((seq, width), lambda j: (0, j)),
            pl.BlockSpec((seq, HD), lambda j: (0, 0)),
            pl.BlockSpec((seq, HD), lambda j: (0, 0)),
        ],
        out_specs=(
            pl.BlockSpec((seq, width), lambda j: (0, j)),
            pl.BlockSpec((2, seq, HD), lambda j: (0, 0, j)),
        ),
        scratch_shapes=[pltpu.VMEM((seq, HD), jnp.float32), pltpu.VMEM((seq, HD), jnp.float32)],
        compiler_params=pltpu.CompilerParams(vmem_limit_bytes=VMEM_LIMIT),
        name="attend",
    )(kv_rows, kv_rows, queries, cotangent, cosine, sine_t)


ORDER = ((1, 0), (0, 1))


def place(dims):
    dp, fs = lax.axis_index("dp"), lax.axis_index("fsdp")
    return (dp // dims[1], dp % dims[1], fs // 2), fs % 2


def target(dims, at, core, axis=None, offset=0):
    at = list(at)
    if axis is not None:
        at[axis] = (at[axis] + offset) % dims[axis]
    return (at[0] * dims[1] + at[1], at[2] * 2 + core)


def greet(peers):
    barrier = pltpu.get_barrier_semaphore()
    for peer in peers:
        pl.semaphore_signal(barrier, inc=1, device_id=peer, device_id_type=MESH)
    pl.semaphore_wait(barrier, len(peers))


def send(src, dst, send_sem, recv_sem, peer):
    return pltpu.make_async_remote_copy(
        src_ref=src, dst_ref=dst, send_sem=send_sem, recv_sem=recv_sem,
        device_id=peer, device_id_type=MESH)


def all_peers(dims, at, core):
    peers = [target(dims, at, core, axis, k) for axis in range(3) for k in range(1, dims[axis])]
    return peers + [target(dims, at, 1 - core)]


def gather_kernel(dims, block_ref, hidden_ref, kv_ref, x2_ref, cos_ref, sin_ref, full, acc, hid, load_sem, x_send, x_recv,
                  recv, z_send, s2, s3, c_send):
    at, core = place(dims)
    depth = dims[2]
    rows, cols = block_ref.shape
    half = rows // 2
    other = target(dims, at, 1 - core)

    def piece(c, h, zz, pos):
        return full.at[c, zz, pos[0], pos[1], pl.ds(h * half, half)]

    def cell(h, zz, pos):
        return recv.at[core, h, zz, pos[0], pos[1]]

    def moved(axis, k):
        pos = [at[0], at[1]]
        pos[axis] = (pos[axis] + k) % dims[axis]
        return pos

    def push(h, zz, pos, send_sem, peer):
        ref = piece(core, h, zz, pos)
        return send(ref, ref, send_sem, cell(h, zz, pos), peer)

    def to_z(h, zz, side):
        return push(h, zz, at[:2], z_send.at[h, side, zz],
                    target(dims, at, core, 2, (1, dims[2] - 1)[side]))

    def sides(act):
        pl.when(at[2] < depth - 1)(lambda: act(0))
        pl.when(at[2] > 0)(lambda: act(1))

    def near(k, act):
        below, above = at[2] - k, at[2] + k
        pl.when(below >= 0)(lambda: act(below, 0))
        pl.when(above < depth)(lambda: act(above, 1))

    def to_second(h, zz, k):
        d2 = ORDER[1 - h][0]
        return push(h, zz, at[:2], s2[h].at[k - 1, zz], target(dims, at, core, d2, k))

    def to_third(h, zz, pos, k):
        d2, d3 = ORDER[1 - h]
        return push(h, zz, pos, s3[h].at[k - 1, zz, pos[d2]], target(dims, at, core, d3, k))

    def to_core(h, zz, pos):
        ref = piece(core, h, zz, pos)
        return send(ref, ref, c_send.at[h, zz, pos[0], pos[1]], cell(h, zz, pos), other)

    def swap(zz):
        src = pl.multiple_of((2 * zz + 1 - core) * rows, rows)
        dst = pl.multiple_of(zz * rows, rows)
        return send(hidden_ref.at[:, pl.ds(src, rows)], x2_ref.at[:, pl.ds(dst, rows)],
                    x_send.at[zz], x_recv.at[zz], other)

    def arrived(c, h, zz, pos):
        ref = piece(c, h, zz, pos)
        send(ref, ref, c_send.at[h, zz, pos[0], pos[1]], recv.at[c, h, zz, pos[0], pos[1]],
             other).wait_recv()

    def relay_first(h, zz):
        d2, d3 = ORDER[1 - h]
        for k in range(1, dims[d2]):
            to_second(h, zz, k).start()
        for k in range(1, dims[d3]):
            to_third(h, zz, at[:2], k).start()
        to_core(h, zz, at[:2]).start()

    def relay_second(zz):
        for h in range(2):
            d2, d3 = ORDER[1 - h]
            for k2 in range(1, dims[d2]):
                pos = moved(d2, k2)
                arrived(core, h, zz, pos)
                for k in range(1, dims[d3]):
                    to_third(h, zz, pos, k).start()
                to_core(h, zz, pos).start()

    def product(c, zz, first):
        x = hid[:, pl.ds(pl.multiple_of((2 * zz + c) * rows, rows), rows)]
        for dp in range(dims[0] * dims[1]):
            w = full[c, zz, dp // dims[1], dp % dims[1]]
            got = mm(x, w)
            if first:
                acc[:, dp * cols:(dp + 1) * cols] = got
            else:
                acc[:, dp * cols:(dp + 1) * cols] += got

    def relay_third(zz):
        for h in range(2):
            d2, d3 = ORDER[1 - h]
            for k3 in range(1, dims[d3]):
                for k2 in range(dims[d2]):
                    pos = moved(d3, k3)
                    pos[d2] = (at[d2] + k2) % dims[d2]
                    arrived(core, h, zz, pos)
                    to_core(h, zz, pos).start()

    def from_core(zz):
        for h in range(2):
            for i in range(dims[0]):
                for j in range(dims[1]):
                    arrived(1 - core, h, zz, (i, j))

    loads = [pltpu.make_async_copy(block_ref.at[pl.ds(h * half, half)], piece(core, h, at[2], at[:2]),
                                   load_sem.at[h]) for h in range(2)]
    for load in loads:
        load.start()
    whole = pltpu.make_async_copy(hidden_ref, hid, load_sem.at[2])
    whole.start()
    greet(all_peers(dims, at, core))
    for load in loads:
        load.wait()
    def start_z(zz, side):
        for h in range(2):
            to_z(h, zz, side).start()

    sides(lambda side: start_z(at[2], side))
    for h in range(2):
        relay_first(h, at[2])

    @pl.loop(0, depth)
    def _(zz):
        swap(zz).start()

    cosine, sine_t = rope_tables(*cos_ref.shape)
    cos_ref[...] = cosine
    sin_ref[...] = sine_t

    def take_z(zz, side):
        for h in range(2):
            arrived(core, h, zz, at[:2])
        more = at[2] < depth - 1 if side == 0 else at[2] > 0
        pl.when(more)(lambda: start_z(zz, side))
        for h in range(2):
            relay_first(h, zz)

    near(1, take_z)
    relay_second(at[2])

    @pl.loop(2, depth)
    def _(k):
        near(k, take_z)
        near(k - 1, lambda zz, side: relay_second(zz))

    near(depth - 1, lambda zz, side: relay_second(zz))

    whole.wait()
    relay_third(at[2])
    product(core, at[2], True)

    def finish_core(zz):
        from_core(zz)
        product(1 - core, zz, False)

    def third_near(zz, side):
        relay_third(zz)
        product(core, zz, False)

    near(1, third_near)
    finish_core(at[2])

    @pl.loop(2, depth)
    def _(k):
        near(k, third_near)
        near(k - 1, lambda zz, side: finish_core(zz))

    near(depth - 1, lambda zz, side: finish_core(zz))
    kv_ref[...] = acc[...].astype(jnp.bfloat16)

    @pl.loop(0, depth)
    def _(zz):
        for h in range(2):
            pl.when((zz <= at[2]) & (at[2] < depth - 1))(lambda: to_z(h, zz, 0).wait_send())
            pl.when((zz >= at[2]) & (at[2] > 0))(lambda: to_z(h, zz, 1).wait_send())

    @pl.loop(0, depth)
    def _(zz):
        swap(zz).wait()
        for h in range(2):
            d2, d3 = ORDER[1 - h]
            for k in range(1, dims[d2]):
                to_second(h, zz, k).wait_send()
            for k in range(1, dims[d3]):
                for k2 in range(dims[d2]):
                    pos = moved(d2, k2)
                    to_third(h, zz, pos, k).wait_send()
            for i in range(dims[0]):
                for j in range(dims[1]):
                    to_core(h, zz, (i, j)).wait_send()


def gather_project(dims, blended, hidden):
    rows, cols = blended.shape
    seq = hidden.shape[0]
    a, b, z = dims
    width = a * b * cols
    sem = pltpu.SemaphoreType.DMA

    def body(*refs):
        gather_kernel(dims, *refs[:14], (refs[14], refs[15]), (refs[16], refs[17]), refs[18])

    def sems(h):
        d2, d3 = ORDER[1 - h]
        return dims[d2], dims[d3]

    vmem = pl.BlockSpec(memory_space=pltpu.VMEM)
    return pl.pallas_call(
        body,
        out_shape=(
            jax.ShapeDtypeStruct((seq, width), jnp.bfloat16),
            jax.ShapeDtypeStruct((seq, z * rows), jnp.bfloat16),
            jax.ShapeDtypeStruct((seq, HD), jnp.float32),
            jax.ShapeDtypeStruct((seq, HD), jnp.float32),
        ),
        in_specs=[pl.BlockSpec(memory_space=pl.ANY)] * 2,
        out_specs=(vmem, pl.BlockSpec(memory_space=pl.ANY), vmem, vmem),
        scratch_shapes=[
            pltpu.VMEM((2, z, a, b, rows, cols), jnp.bfloat16),
            pltpu.VMEM((seq, width), jnp.float32),
            pltpu.VMEM(hidden.shape, hidden.dtype),
            sem((3,)), sem((z,)), sem((z,)),
            sem((2, 2, z, a, b)),
            sem((2, 2, z)),
            *[sem((sems(h)[0] - 1, z)) for h in range(2)],
            *[sem((sems(h)[1] - 1, z, sems(h)[0])) for h in range(2)],
            sem((2, z, a, b)),
        ],
        compiler_params=pltpu.CompilerParams(
            collective_id=2, has_side_effects=True, vmem_limit_bytes=VMEM_LIMIT),
        name="gather_project",
    )(blended, hidden)


def reduce_kernel(dims, h_ref, x2_ref, y1_ref, out_ref, y2_ref, swap_send, swap_recv, xs, xsem, early,
                  *scratch):
    halves = [scratch[:11], scratch[11:]]
    at, core = place(dims)
    depth = dims[2]
    rows, cols = out_ref.shape
    half = rows // 2
    parts = y1_ref.shape[0]
    width = y1_ref.shape[2]
    other = target(dims, at, 1 - core)
    def loads(zz):
        own = pl.multiple_of((2 * zz + core) * rows, rows)
        theirs = pl.multiple_of(zz * rows, rows)
        return (pltpu.make_async_copy(h_ref.at[:, pl.ds(own, rows)], xs.at[0, zz], xsem.at[0, zz]),
                pltpu.make_async_copy(x2_ref.at[:, pl.ds(theirs, rows)], xs.at[1, zz], xsem.at[1, zz]))

    @pl.loop(1, depth + 1)
    def _(step):
        for load in loads((at[2] + step) % depth):
            load.start()

    greet(all_peers(dims, at, core))
    swap = send(y1_ref, y2_ref, swap_send, swap_recv, other)
    swap.start()

    def first_copy(h, k1, zz):
        d1 = ORDER[h][0]
        part, r1, s1, q1 = halves[h][0], halves[h][1], halves[h][5], halves[h][6]
        v1 = (at[d1] + k1) % dims[d1]
        return send(part.at[zz, v1], r1.at[k1 - 1, zz], s1.at[k1 - 1, zz], q1.at[k1 - 1, zz],
                    target(dims, at, core, d1, k1))

    def second_copy(h, k2, zz):
        d2 = ORDER[h][1]
        sum2, r2, s2, q2 = halves[h][2], halves[h][3], halves[h][7], halves[h][8]
        return send(sum2.at[k2 - 1, zz], r2.at[k2 - 1, zz], s2.at[k2 - 1, zz], q2.at[k2 - 1, zz],
                    target(dims, at, core, d2, k2))

    def third_copy(h, k):
        r3, s3, q3 = halves[h][4], halves[h][9], halves[h][10]
        part = halves[h][0]
        zz = (at[2] + k) % depth
        d1, d2 = ORDER[h]
        return send(part.at[zz, at[d1], at[d2]], r3.at[k - 1], s3.at[k - 1], q3.at[k - 1],
                    target(dims, at, core, 2, k))

    def compute(step, peeled=False):
        zz = (at[2] + step) % depth
        own, theirs = loads(zz)
        if not peeled:
            own.wait()
        theirs.wait()
        for part in range(parts):
            first = early[part] if peeled else mm(xs[0, zz], y1_ref[part], TN)
            r = (first + mm(xs[1, zz], y2_ref[part], TN)).astype(jnp.bfloat16)
            for i in range(width // cols):
                dp = part * (width // cols) + i
                where = (dp // dims[1], dp % dims[1])
                for h in range(2):
                    d1, d2 = ORDER[h]
                    halves[h][0][zz, where[d1], where[d2]] = (
                        r[h * half:(h + 1) * half, i * cols:(i + 1) * cols])
        for h in range(2):
            for k1 in range(1, dims[ORDER[h][0]]):
                first_copy(h, k1, zz).start()

    def keep1(h, zz, v2):
        d1, d2 = ORDER[h]
        part, r1 = halves[h][0], halves[h][1]
        total = part[zz, at[d1], v2].astype(jnp.float32)
        for k1 in range(1, dims[d1]):
            total += r1[k1 - 1, zz, v2].astype(jnp.float32)
        return total

    def second(step):
        zz = (at[2] + step) % depth
        for h in range(2):
            d1, d2 = ORDER[h]
            for k1 in range(1, dims[d1]):
                first_copy(h, k1, zz).wait_recv()
            for k2 in range(1, dims[d2]):
                v2 = (at[d2] + k2) % dims[d2]
                halves[h][2][k2 - 1, zz] = keep1(h, zz, v2).astype(jnp.bfloat16)
                second_copy(h, k2, zz).start()

    def keep2(h, zz):
        d1, d2 = ORDER[h]
        total = keep1(h, zz, at[d2])
        for k2 in range(1, dims[d2]):
            second_copy(h, k2, zz).wait_recv()
        for k2 in range(1, dims[d2]):
            total += halves[h][3][k2 - 1, zz].astype(jnp.float32)
        return total

    def third(step):
        zz = (at[2] + step) % depth
        for h in range(2):
            d1, d2 = ORDER[h]
            halves[h][0][zz, at[d1], at[d2]] = keep2(h, zz).astype(jnp.bfloat16)
            third_copy(h, step).start()

    start = (at[2] + 1) % depth
    loads(start)[0].wait()
    for part in range(parts):
        early[part] = mm(xs[0, start], y1_ref[part], TN)
    swap.wait()
    compute(1, True)
    compute(2)
    second(1)

    @pl.loop(3, depth + 1)
    def _(step):
        compute(step)
        second(step - 1)
        third(step - 2)

    second(depth)
    third(depth - 1)

    for h in range(2):
        total = keep2(h, at[2])
        for k in range(1, depth):
            third_copy(h, k).wait_recv()
            total += halves[h][4][k - 1].astype(jnp.float32)
        out_ref[h * half:(h + 1) * half] = total

    @pl.loop(0, depth)
    def _(zz):
        for h in range(2):
            for k1 in range(1, dims[ORDER[h][0]]):
                first_copy(h, k1, zz).wait_send()
            for k2 in range(1, dims[ORDER[h][1]]):
                second_copy(h, k2, zz).wait_send()

    @pl.loop(1, depth)
    def _(k):
        for h in range(2):
            third_copy(h, k).wait_send()


def reduce_gradient(dims, x1, x2, y1, rows, cols):
    half = rows // 2
    scratch = [
        pltpu.VMEM(y1.shape, y1.dtype), pltpu.SemaphoreType.DMA, pltpu.SemaphoreType.DMA,
        pltpu.VMEM((2, dims[2], y1.shape[1], rows), jnp.bfloat16),
        pltpu.SemaphoreType.DMA((2, dims[2])),
        pltpu.VMEM((y1.shape[0], rows, y1.shape[2]), jnp.float32),
    ]
    for h in range(2):
        n1, n2 = dims[ORDER[h][0]], dims[ORDER[h][1]]
        z = dims[2]
        scratch += [
            pltpu.VMEM((z, n1, n2, half, cols), jnp.bfloat16),
            pltpu.VMEM((n1 - 1, z, n2, half, cols), jnp.bfloat16),
            pltpu.VMEM((n2 - 1, z, half, cols), jnp.bfloat16),
            pltpu.VMEM((n2 - 1, z, half, cols), jnp.bfloat16),
            pltpu.VMEM((z - 1, half, cols), jnp.bfloat16),
            pltpu.SemaphoreType.DMA((n1 - 1, z)), pltpu.SemaphoreType.DMA((n1 - 1, z)),
            pltpu.SemaphoreType.DMA((n2 - 1, z)), pltpu.SemaphoreType.DMA((n2 - 1, z)),
            pltpu.SemaphoreType.DMA((z - 1,)), pltpu.SemaphoreType.DMA((z - 1,)),
        ]
    vmem = pl.BlockSpec(memory_space=pltpu.VMEM)
    return pl.pallas_call(
        functools.partial(reduce_kernel, dims),
        out_shape=jax.ShapeDtypeStruct((rows, cols), jnp.float32),
        in_specs=[pl.BlockSpec(memory_space=pl.ANY)] * 2 + [vmem],
        out_specs=vmem,
        scratch_shapes=scratch,
        compiler_params=pltpu.CompilerParams(
            collective_id=1, has_side_effects=True, vmem_limit_bytes=VMEM_LIMIT),
        name="reduce_gradient",
    )(x1, x2, y1)


def local(dims, hidden, queries, cotangent, point_start, point_mid, point_end, curve_time):
    t_value = curve_time[0]
    blended = (
        (1.0 - t_value) ** 2 * point_start.astype(jnp.float32)
        + 2.0 * t_value * (1.0 - t_value) * point_mid.astype(jnp.float32)
        + t_value**2 * point_end.astype(jnp.float32)
    ).astype(jnp.bfloat16)
    rows, cols = point_mid.shape
    kv_rows, x2, cosine, sine_t = gather_project(dims, blended, hidden)
    context, kv_grad = attend(kv_rows, queries, cotangent, cosine, sine_t)
    gradient = reduce_gradient(dims, hidden, x2, kv_grad, rows, cols)
    return (context, gradient * (2.0 * t_value * (1.0 - t_value)))


def solution(mesh):
    dp, fsdp = mesh.shape["dp"], mesh.shape["fsdp"]
    dims = (dp // 2, 2, fsdp // 2)
    return jax.shard_map(
        functools.partial(local, dims),
        mesh=mesh,
        in_specs=(
            P(("dp", "fsdp"), None),
            P(("dp", "fsdp"), None),
            P(("dp", "fsdp"), None),
            P("fsdp", "dp"),
            P("fsdp", "dp"),
            P("fsdp", "dp"),
            P(),
        ),
        out_specs=(P(("dp", "fsdp"), None), P("fsdp", "dp")),
        check_vma=False,
    )
```

profile of v0, /device:TPU:0, one launch (start us, length us, event | category | flops | bytes accessed | tf_op | source)
XLA Modules:
  0.0 119.3 jit_solution(9836521020588678262)
XLA Ops:
  1.3 2.0 %add_convert_fusion.refs_0_ = bf16[512,256]{1,0:T(8,128)(2,1)} fusion(bf16[512,256]{1,0:T(8,128)(2,1)} %param.12, bf16[512,256]{1,0:T(8,128)(2,1)} %param.11, bf16[512,256]{1,0:T(8,128)(2,1)} %param.10, f32[]{:T(128)} %bitcast.2, f32[]{:T(128)} %bitcast.1, f32[]{:T(128)} %bitcast), kind=kLoop, calls=%fused_computation | loop fusion | flops 1179648 | bytes 1048588 | tf_op jit(solution)/shard_map/convert_element_type | solution.py:563
  3.2 46.8 %gather_project.1 = (bf16[512,1024]{1,0:T(8,128)(2,1)}, bf16[512,2048]{1,0:T(8,128)(2,1)}, f32[512,128]{1,0:T(8,128)}, f32[512,128]{1,0:T(8,128)}) custom-call(bf16[512,256]{1,0:T(8,128)(2,1)} %add_convert_fusion.refs_0_, bf16[512,4096]{1,0:T(8,128)(2,1)} %h_ref.1), custom_call_target="tpu_custom_call" | custom-call | tf_op jit(solution)/shard_map/gather_project/pallas_call | solution.py:356
  50.0 15.9 %attend.1 = (bf16[512,2048]{1,0:T(8,128)(2,1)}, bf16[2,512,512]{2,1,0:T(8,128)(2,1)}) custom-call(bf16[512,1024]{1,0:T(8,128)(2,1)} %get-tuple-element.8.k_ref.v_ref, bf16[512,1024]{1,0:T(8,128)(2,1)} %get-tuple-element.8.k_ref.v_ref, bf16[512,2048]{1,0:T(8,128)(2,1)} %q_ref.1, bf16[512,2048]{1,0:T(8,128)(2,1)} %g_ref.1, ...), custom_call_target="tpu_custom_call" | custom-call | tf_op jit(solution)/shard_map/attend/pallas_call | solution.py:92
  65.9 51.5 %reduce_gradient.1 = f32[512,256]{1,0:T(8,128)} custom-call(bf16[512,4096]{1,0:T(8,128)(2,1)} %h_ref.1, bf16[512,2048]{1,0:T(8,128)(2,1)} %get-tuple-element.12.x2_ref, bf16[2,512,512]{2,1,0:T(8,128)(2,1)} %get-tuple-element.13.y1_ref), custom_call_target="tpu_custom_call" | custom-call | tf_op jit(solution)/shard_map/reduce_gradient/pallas_call | solution.py:545
  117.5 1.9 %broadcast_multiply_fusion = f32[512,256]{1,0:T(8,128)} fusion(f32[512,256]{1,0:T(8,128)} %reduce_gradient.1, f32[]{:T(128)} %bitcast.1), kind=kLoop, calls=%fused_computation.1 | loop fusion | flops 131072 | bytes 1048580 | tf_op jit(solution)/shard_map/mul | solution.py:568
where the time goes:
time: 120 us; the launch traced here: 119 us
  Pallas kernels  114 us (95%)
  other arithmetic  3.83 us (3%)
  between operations  1.3 us (1%)
    pallas_call x1, Pallas kernels, reduce_gradient(): pl.pallas_call(functools.partial(reduce_kernel, dims), out_shape=jax.Shap...  51.5 us
    pallas_call x1, Pallas kernels, gather_project(): pl.pallas_call(body, out_shape=(jax.ShapeDtypeStruct((seq, width), jnp.bf...  46.8 us
    pallas_call x1, Pallas kernels, attend(): pl.pallas_call(attend_kernel, grid=(heads,), out_shape=(jax.ShapeDtypeStr...  15.9 us

commit v1 on v0

v1 whole, which is shorter than its diff:
```python
import functools
import math

import jax
import jax.numpy as jnp
from jax import lax
from jax.experimental import pallas as pl
from jax.experimental.pallas import tpu as pltpu
from jax.sharding import PartitionSpec as P

HD = 128
BQ = 256
MESH = pl.DeviceIdType.MESH
VMEM_LIMIT = 60 * 1024 * 1024


def rope_tables(seq_len, head_dim):
    shape = (seq_len, head_dim)
    positions = lax.broadcasted_iota(jnp.int32, shape, 0).astype(jnp.float32)
    column = lax.broadcasted_iota(jnp.int32, shape, 1)
    halves_index = jnp.where(column < head_dim // 2, column, column - head_dim // 2).astype(jnp.float32)
    inverse = jnp.exp(-(2.0 * halves_index / head_dim) * math.log(500000.0))
    angles = positions * inverse
    cosine, sine_t = jnp.cos(angles), jnp.sin(angles)
    return (cosine, sine_t)


def rotate(x):
    half = x.shape[-1] // 2
    return jnp.concatenate([-x[..., half:], x[..., :half]], axis=-1)


def rotate_back(x):
    half = x.shape[-1] // 2
    return jnp.concatenate([x[..., half:], -x[..., :half]], axis=-1)


NN = (((1,), (0,)), ((), ()))
NT = (((1,), (1,)), ((), ()))
TN = (((0,), (0,)), ((), ()))


def mm(x, y, dims=NN):
    return lax.dot_general(x, y, dims, preferred_element_type=jnp.float32)


ORDER = ((1, 0), (0, 1))


def place(dims):
    dp, fs = lax.axis_index("dp"), lax.axis_index("fsdp")
    return (dp // dims[1], dp % dims[1], fs // 2), fs % 2


def target(dims, at, core, axis=None, offset=0):
    at = list(at)
    if axis is not None:
        at[axis] = (at[axis] + offset + dims[axis]) % dims[axis]
    return (at[0] * dims[1] + at[1], at[2] * 2 + core)


def send(src, dst, send_sem, recv_sem, peer):
    return pltpu.make_async_remote_copy(
        src_ref=src, dst_ref=dst, send_sem=send_sem, recv_sem=recv_sem,
        device_id=peer, device_id_type=MESH)


def all_peers(dims, at, core):
    peers = [target(dims, at, core, axis, k) for axis in range(3) for k in range(1, dims[axis])]
    return peers + [target(dims, at, 1 - core)]


def attend_head(keys_at, values_at, q_cols, kv, q_ref, g_ref, cos_ref, sin_ref, ctx_ref, y_ref, kg, vg):
    seq = kv.shape[0]
    group = q_cols[1] // HD
    scale = 1.0 / math.sqrt(HD)
    to_base2 = scale * math.log2(math.e)

    def cols(g):
        return pl.ds(pl.multiple_of(q_cols[0] + g * HD, HD), HD)

    raw = kv[:, keys_at].astype(jnp.float32)
    cosine, sine_t = cos_ref[...], sin_ref[...]
    keys = (raw * cosine + rotate(raw) * sine_t).astype(jnp.bfloat16)
    values = kv[:, values_at]
    values_t = values.astype(jnp.float32).T.astype(jnp.bfloat16)
    kg[...] = jnp.zeros_like(kg)
    vg[...] = jnp.zeros_like(vg)
    for start in range(0, seq, BQ):
        nk = start + BQ
        rows = slice(start, nk)
        qs = jnp.concatenate([q_ref[rows, cols(g)] for g in range(group)], axis=0)
        gs = jnp.concatenate([g_ref[rows, cols(g)] for g in range(group)], axis=0)
        s = mm(keys[:nk], qs, NT)
        key_at = lax.broadcasted_iota(jnp.int32, (BQ, group * BQ), 0)
        query_at = lax.broadcasted_iota(jnp.int32, (BQ, group * BQ), 1) % BQ
        last = jnp.where(key_at <= query_at, s[start:], -1e30)
        s = last if start == 0 else jnp.concatenate([s[:start], last], axis=0)
        top = jnp.max(s, axis=0, keepdims=True)
        w = jnp.exp2((s - top) * to_base2)
        p = w * (1.0 / jnp.sum(w, axis=0, keepdims=True))
        p_low = p.astype(jnp.bfloat16)
        ctx_t = mm(values_t[:, :nk], p_low)
        dp = mm(values[:nk], gs, NT)
        vg[:nk] += mm(p_low, gs)
        delta = jnp.sum(dp * p, axis=0, keepdims=True)
        ds = (p * ((dp - delta) * scale)).astype(jnp.bfloat16)
        kg[:nk] += mm(ds, qs)
        ctx = ctx_t.T.astype(jnp.bfloat16)
        for g in range(group):
            ctx_ref[rows, cols(g)] = ctx[g * BQ:(g + 1) * BQ]
    rot = kg[...]
    y_ref[:, keys_at] = (rot * cosine + rotate_back(rot * sine_t)).astype(jnp.bfloat16)
    y_ref[:, values_at] = vg[...].astype(jnp.bfloat16)


def step_kernel(dims, t_ref, start_ref, mid_ref, end_ref, hidden_ref, query_ref, cot_ref, out_ctx, out_ref,
                pts, hid, x2, qv, gv, ctx, cos_ref, sin_ref, full, acc, kv, kg, vg, y1, y2, early,
                load_sem, x_send, x_recv, recv, z_send, c_send, y_send, y_recv, *more):
    s2, s3 = more[:2], more[2:4]
    halves = [more[4:15], more[15:26]]
    at, core = place(dims)
    depth = dims[2]
    across = dims[0] * dims[1]
    rows = start_ref.shape[0]
    half = rows // 2
    groups = full.shape[0]
    heads = across // 2
    other = target(dims, at, 1 - core)
    here = at[:2]


    def piece(p, c, h, zz, pos):
        col = pl.multiple_of((pos[0] * dims[1] + pos[1]) * HD, HD)
        return full.at[p, c, zz, pl.ds(h * half, half), pl.ds(col, HD)]

    def moved(axis, k):
        pos = [at[0], at[1]]
        pos[axis] = (pos[axis] + k) % dims[axis]
        return pos

    def push(p, h, zz, pos, send_sem, peer):
        ref = piece(p, core, h, zz, pos)
        return send(ref, ref, send_sem, recv.at[p, core, h, zz, pos[0], pos[1]], peer)

    def to_z(p, h, zz, side):
        return push(p, h, zz, here, z_send.at[p, h, side, zz], target(dims, at, core, 2, 1 - 2 * side))

    def onward(side):
        return ((side == 0) & (at[2] < depth - 1)) | ((side == 1) & (at[2] > 0))

    def near(k, act):
        @pl.loop(0, 2)
        def _(side):
            zz = at[2] + (2 * side - 1) * k
            pl.when((zz >= 0) & (zz < depth))(lambda: act(zz, side))

    def to_second(p, h, zz, k):
        d2 = ORDER[1 - h][0]
        return push(p, h, zz, here, s2[h].at[p, k - 1, zz], target(dims, at, core, d2, k))

    def to_third(p, h, zz, pos, k):
        d2, d3 = ORDER[1 - h]
        return push(p, h, zz, pos, s3[h].at[p, k - 1, zz, pos[d2]], target(dims, at, core, d3, k))

    def to_core(p, h, zz, pos):
        ref = piece(p, core, h, zz, pos)
        return send(ref, ref, c_send.at[p, h, zz, pos[0], pos[1]],
                    recv.at[p, core, h, zz, pos[0], pos[1]], other)

    def swap_x(zz):
        src = pl.multiple_of((2 * zz + 1 - core) * rows, rows)
        dst = pl.multiple_of(zz * rows, rows)
        return send(hidden_ref.at[:, pl.ds(src, rows)], x2.at[:, pl.ds(dst, rows)],
                    x_send.at[zz], x_recv.at[zz], other)

    def arrived(p, c, h, zz, pos):
        ref = piece(p, c, h, zz, pos)
        send(ref, ref, c_send.at[p, h, zz, pos[0], pos[1]], recv.at[p, c, h, zz, pos[0], pos[1]],
             other).wait_recv()

    def send_second(p, h, zz):
        for k in range(1, dims[ORDER[1 - h][0]]):
            to_second(p, h, zz, k).start()

    def send_own(p, h, zz):
        for k in range(1, dims[ORDER[1 - h][1]]):
            to_third(p, h, zz, here, k).start()
        to_core(p, h, zz, here).start()

    def start_z(p, zz, side):
        for h in range(2):
            to_z(p, h, zz, side).start()

    def own_z(p):
        @pl.loop(0, 2)
        def _(side):
            pl.when(onward(side))(lambda: start_z(p, at[2], side))

    def take_z(p, zz, side):
        for h in range(2):
            arrived(p, core, h, zz, here)
            pl.when(onward(side))(lambda: to_z(p, h, zz, side).start())
            if p == 0:
                send_second(p, h, zz)
                send_own(p, h, zz)

    def relay_second(p, zz):
        for h in range(2):
            d2, d3 = ORDER[1 - h]
            for k2 in range(1, dims[d2]):
                pos = moved(d2, k2)
                arrived(p, core, h, zz, pos)
                for k in range(1, dims[d3]):
                    to_third(p, h, zz, pos, k).start()
                to_core(p, h, zz, pos).start()

    def product(p, c, zz, first=False):
        x = hid[:, pl.ds(pl.multiple_of((2 * zz + c) * rows, rows), rows)]
        got = mm(x, full[p, c, zz])
        if first:
            acc[...] = got
        else:
            acc[...] += got

    def third(p, zz, first=False):
        for h in range(2):
            d2, d3 = ORDER[1 - h]
            for k3 in range(1, dims[d3]):
                for k2 in range(dims[d2]):
                    pos = moved(d3, k3)
                    pos[d2] = (at[d2] + k2) % dims[d2]
                    arrived(p, core, h, zz, pos)
                    to_core(p, h, zz, pos).start()
        product(p, core, zz, first)

    def from_core(p, zz):
        for h in range(2):
            for i in range(dims[0]):
                for j in range(dims[1]):
                    arrived(p, 1 - core, h, zz, (i, j))
        product(p, 1 - core, zz)

    def drain_gather():
        for p in range(groups):
            @pl.loop(0, depth)
            def _(zz):
                for h in range(2):
                    pl.when((zz <= at[2]) & (at[2] < depth - 1))(lambda: to_z(p, h, zz, 0).wait_send())
                    pl.when((zz >= at[2]) & (at[2] > 0))(lambda: to_z(p, h, zz, 1).wait_send())
                    d2, d3 = ORDER[1 - h]
                    for k in range(1, dims[d2]):
                        to_second(p, h, zz, k).wait_send()
                    for k in range(1, dims[d3]):
                        for k2 in range(dims[d2]):
                            to_third(p, h, zz, moved(d2, k2), k).wait_send()
                    for i in range(dims[0]):
                        for j in range(dims[1]):
                            to_core(p, h, zz, (i, j)).wait_send()


    def first_copy(p, h, k1, zz):
        d1 = ORDER[h][0]
        part, r1, s1, q1 = halves[h][0], halves[h][1], halves[h][5], halves[h][6]
        v1 = (at[d1] + k1) % dims[d1]
        return send(part.at[p, zz, v1], r1.at[p, k1 - 1, zz], s1.at[p, k1 - 1, zz], q1.at[p, k1 - 1, zz],
                    target(dims, at, core, d1, k1))

    def second_copy(p, h, k2, zz):
        d2 = ORDER[h][1]
        sum2, r2, t2, q2 = halves[h][2], halves[h][3], halves[h][7], halves[h][8]
        return send(sum2.at[p, k2 - 1, zz], r2.at[p, k2 - 1, zz], t2.at[p, k2 - 1, zz],
                    q2.at[p, k2 - 1, zz], target(dims, at, core, d2, k2))

    def third_copy(p, h, k):
        part, r3, t3, q3 = halves[h][0], halves[h][4], halves[h][9], halves[h][10]
        zz = (at[2] + k) % depth
        d1, d2 = ORDER[h]
        return send(part.at[p, zz, at[d1], at[d2]], r3.at[p, k - 1], t3.at[p, k - 1], q3.at[p, k - 1],
                    target(dims, at, core, 2, k))

    def swap_y(p):
        return send(y1.at[p], y2.at[p], y_send.at[p], y_recv.at[p], other)

    def partial_own(p):
        @pl.loop(0, depth)
        def _(zz):
            x = hid[:, pl.ds(pl.multiple_of((2 * zz + core) * rows, rows), rows)]
            early[zz] = mm(x, y1[p], TN)

    def partial_send(p):
        @pl.loop(1, depth + 1)
        def _(step):
            zz = (at[2] + step) % depth
            if p == 0:
                swap_x(zz).wait_recv()
            x = x2[:, pl.ds(pl.multiple_of(zz * rows, rows), rows)]
            r = (early[zz] + mm(x, y2[p], TN)).astype(jnp.bfloat16)
            for dp in range(across):
                where = (dp // dims[1], dp % dims[1])
                for h in range(2):
                    d1, d2 = ORDER[h]
                    halves[h][0][p, zz, where[d1], where[d2]] = (
                        r[h * half:(h + 1) * half, dp * HD:(dp + 1) * HD])
            for h in range(2):
                for k1 in range(1, dims[ORDER[h][0]]):
                    first_copy(p, h, k1, zz).start()

    def keep1(p, h, zz, v2):
        d1, d2 = ORDER[h]
        part, r1 = halves[h][0], halves[h][1]
        total = part[p, zz, at[d1], v2].astype(jnp.float32)
        for k1 in range(1, dims[d1]):
            total += r1[p, k1 - 1, zz, v2].astype(jnp.float32)
        return total

    def sum_second(p, step):
        zz = (at[2] + step) % depth
        for h in range(2):
            d1, d2 = ORDER[h]
            for k1 in range(1, dims[d1]):
                first_copy(p, h, k1, zz).wait_recv()
            for k2 in range(1, dims[d2]):
                v2 = (at[d2] + k2) % dims[d2]
                halves[h][2][p, k2 - 1, zz] = keep1(p, h, zz, v2).astype(jnp.bfloat16)
                second_copy(p, h, k2, zz).start()

    def keep2(p, h, zz):
        d1, d2 = ORDER[h]
        total = keep1(p, h, zz, at[d2])
        for k2 in range(1, dims[d2]):
            second_copy(p, h, k2, zz).wait_recv()
        for k2 in range(1, dims[d2]):
            total += halves[h][3][p, k2 - 1, zz].astype(jnp.float32)
        return total

    def sum_third(p, step):
        zz = (at[2] + step) % depth
        for h in range(2):
            d1, d2 = ORDER[h]
            halves[h][0][p, zz, at[d1], at[d2]] = keep2(p, h, zz).astype(jnp.bfloat16)
            third_copy(p, h, step).start()

    def finish(p):
        for h in range(2):
            total = keep2(p, h, at[2])
            for k in range(1, depth):
                third_copy(p, h, k).wait_recv()
                total += halves[h][4][p, k - 1].astype(jnp.float32)
            out_ref[h * half:(h + 1) * half, p * HD:(p + 1) * HD] = total

    def drain_reduce(p):
        @pl.loop(0, depth)
        def _(zz):
            for h in range(2):
                for k1 in range(1, dims[ORDER[h][0]]):
                    first_copy(p, h, k1, zz).wait_send()
                for k2 in range(1, dims[ORDER[h][1]]):
                    second_copy(p, h, k2, zz).wait_send()

        @pl.loop(1, depth)
        def _(k):
            for h in range(2):
                third_copy(p, h, k).wait_send()


    points = [pltpu.make_async_copy(ref, pts.at[i], load_sem.at[i])
              for i, ref in enumerate((start_ref, mid_ref, end_ref))]
    wholes = [pltpu.make_async_copy(ref, dst, load_sem.at[3 + i])
              for i, (ref, dst) in enumerate(((hidden_ref, hid), (query_ref, qv), (cot_ref, gv)))]
    for load in points + wholes:
        load.start()
    barrier = pltpu.get_barrier_semaphore()
    peers = all_peers(dims, at, core)
    for peer in peers:
        pl.semaphore_signal(barrier, inc=1, device_id=peer, device_id_type=MESH)
    for load in points:
        load.wait()
    t_value = t_ref[0]
    blended = (
        (1.0 - t_value) * (1.0 - t_value) * pts[0].astype(jnp.float32)
        + 2.0 * t_value * (1.0 - t_value) * pts[1].astype(jnp.float32)
        + t_value * t_value * pts[2].astype(jnp.float32)
    ).astype(jnp.bfloat16)
    col = pl.multiple_of((at[0] * dims[1] + at[1]) * HD, HD)
    for p in range(groups):
        full[p, core, at[2], :, pl.ds(col, HD)] = blended[:, p * HD:(p + 1) * HD]
    pl.semaphore_wait(barrier, len(peers))

    own_z(0)
    for h in range(2):
        send_second(0, h, at[2])
        send_own(0, h, at[2])

    @pl.loop(0, depth)
    def _(zz):
        swap_x(zz).start()

    cosine, sine_t = rope_tables(*cos_ref.shape)
    cos_ref[...] = cosine
    sin_ref[...] = sine_t

    near(1, lambda zz, side: take_z(0, zz, side))
    for p in range(1, groups):
        own_z(p)
    relay_second(0, at[2])
    wholes[0].wait()

    @pl.loop(2, depth)
    def _(k):
        near(k, lambda zz, side: take_z(0, zz, side))
        for p in range(1, groups):
            near(k - 1, lambda zz, side: take_z(p, zz, side))
        near(k - 1, lambda zz, side: relay_second(0, zz))
        pl.when(k == 2)(lambda: third(0, at[2], True))
        pl.when(k > 2)(lambda: near(k - 2, lambda zz, side: third(0, zz)))

    for p in range(1, groups):
        near(depth - 1, lambda zz, side: take_z(p, zz, side))
    near(depth - 1, lambda zz, side: relay_second(0, zz))

    def around(act):
        @pl.loop(0, depth)
        def _(i):
            act((at[2] + i) % depth)

    def send_group(p):
        around(lambda zz: [send_second(p, h, zz) for h in range(2)])
        around(lambda zz: [send_own(p, h, zz) for h in range(2)])

    if groups > 1:
        send_group(1)
    near(depth - 2, lambda zz, side: third(0, zz))
    from_core(0, at[2])

    @pl.loop(1, depth - 2)
    def _(k):
        near(k, lambda zz, side: from_core(0, zz))

    near(depth - 1, lambda zz, side: third(0, zz))
    near(depth - 2, lambda zz, side: from_core(0, zz))
    near(depth - 1, lambda zz, side: from_core(0, zz))
    wholes[1].wait()
    wholes[2].wait()

    share = depth // heads
    for p in range(groups):
        if p > 0:
            around(lambda zz: third(p, zz))
            around(lambda zz: from_core(p, zz))
        kv[...] = acc[...].astype(jnp.bfloat16)
        if p + 1 < groups:
            acc[...] = jnp.zeros_like(acc)

        @pl.loop(0, heads)
        def _(d):
            keys_at = pl.ds(pl.multiple_of(d * HD, HD), HD)
            values_at = pl.ds(pl.multiple_of((heads + d) * HD, HD), HD)
            width = qv.shape[1] // (heads * groups)
            attend_head(keys_at, values_at, ((d * groups + p) * width, width), kv, qv, gv, cos_ref,
                        sin_ref, ctx, y1.at[p], kg, vg)
            if p + 1 < groups:
                @pl.loop(0, share)
                def _(i):
                    relay_second(p + 1, (at[2] + d * share + i) % depth)
            if p > 0:
                @pl.when(d < heads - 1)
                def _():
                    @pl.loop(0, share)
                    def _(i):
                        sum_second(p - 1, d * share + i + 1)

        swap_y(p).start()
        if p == groups - 1:
            context = pltpu.make_async_copy(ctx, out_ctx, load_sem.at[6])
            context.start()
        if p + 2 < groups:
            send_group(p + 2)
        partial_own(p)
        if p > 0:
            @pl.loop((heads - 1) * share + 1, depth + 1)
            def _(step):
                sum_second(p - 1, step)
        swap_y(p).wait()
        partial_send(p)
        if p > 0:
            @pl.loop(1, depth)
            def _(step):
                sum_third(p - 1, step)

    drain_gather()
    last = groups - 1
    sum_second(last, 1)

    @pl.loop(2, depth + 1)
    def _(step):
        sum_second(last, step)
        sum_third(last, step - 1)

    for p in range(groups):
        finish(p)
    for p in range(groups):
        drain_reduce(p)

    @pl.loop(0, depth)
    def _(zz):
        swap_x(zz).wait_send()

    context.wait()


def run_step(dims, hidden, queries, cotangent, point_start, point_mid, point_end, curve_time):
    rows, cols = point_mid.shape
    seq = hidden.shape[0]
    a, b, z = dims
    groups = cols // HD
    half = rows // 2
    width = a * b * HD
    sem = pltpu.SemaphoreType.DMA

    def vm(*shape, dtype=jnp.bfloat16):
        return pltpu.VMEM(shape, dtype)

    f32 = jnp.float32
    scratch = [
        vm(3, rows, cols), vm(*hidden.shape), vm(seq, z * rows), vm(*queries.shape), vm(*cotangent.shape),
        vm(*queries.shape), vm(seq, HD, dtype=f32), vm(seq, HD, dtype=f32),
        vm(groups, 2, z, rows, width), vm(seq, width, dtype=f32), vm(seq, width),
        vm(seq, HD, dtype=f32), vm(seq, HD, dtype=f32),
        vm(groups, seq, width), vm(groups, seq, width), vm(z, rows, width, dtype=f32),
        sem((7,)), sem((z,)), sem((z,)), sem((groups, 2, 2, z, a, b)), sem((groups, 2, 2, z)),
        sem((groups, 2, z, a, b)), sem((groups,)), sem((groups,)),
    ]
    sizes = [[dims[axis] for axis in ORDER[1 - h]] for h in range(2)]
    scratch += [sem((groups, sizes[h][0] - 1, z)) for h in range(2)]
    scratch += [sem((groups, sizes[h][1] - 1, z, sizes[h][0])) for h in range(2)]
    for h in range(2):
        n1, n2 = dims[ORDER[h][0]], dims[ORDER[h][1]]
        scratch += [
            vm(groups, z, n1, n2, half, HD), vm(groups, n1 - 1, z, n2, half, HD),
            vm(groups, n2 - 1, z, half, HD), vm(groups, n2 - 1, z, half, HD),
            vm(groups, z - 1, half, HD),
            sem((groups, n1 - 1, z)), sem((groups, n1 - 1, z)),
            sem((groups, n2 - 1, z)), sem((groups, n2 - 1, z)),
            sem((groups, z - 1)), sem((groups, z - 1)),
        ]
    hbm = pl.BlockSpec(memory_space=pl.ANY)
    vmem = pl.BlockSpec(memory_space=pltpu.VMEM)
    return pl.pallas_call(
        functools.partial(step_kernel, dims),
        out_shape=(
            jax.ShapeDtypeStruct(queries.shape, jnp.bfloat16),
            jax.ShapeDtypeStruct((rows, cols), f32),
        ),
        in_specs=[pl.BlockSpec(memory_space=pltpu.SMEM)] + [hbm] * 6,
        out_specs=(hbm, vmem),
        scratch_shapes=scratch,
        compiler_params=pltpu.CompilerParams(
            collective_id=1, has_side_effects=True, vmem_limit_bytes=VMEM_LIMIT),
        name="bezier_step",
    )(curve_time, point_start, point_mid, point_end, hidden, queries, cotangent)


def local(dims, hidden, queries, cotangent, point_start, point_mid, point_end, curve_time):
    t_value = curve_time[0]
    context, gradient = run_step(dims, hidden, queries, cotangent, point_start, point_mid, point_end, curve_time)
    return (context, gradient * (2.0 * t_value * (1.0 - t_value)))


def solution(mesh):
    dp, fsdp = mesh.shape["dp"], mesh.shape["fsdp"]
    dims = (dp // 2, 2, fsdp // 2)
    return jax.shard_map(
        functools.partial(local, dims),
        mesh=mesh,
        in_specs=(
            P(("dp", "fsdp"), None),
            P(("dp", "fsdp"), None),
            P(("dp", "fsdp"), None),
            P("fsdp", "dp"),
            P("fsdp", "dp"),
            P("fsdp", "dp"),
            P(),
        ),
        out_specs=(P(("dp", "fsdp"), None), P("fsdp", "dp")),
        check_vma=False,
    )
```

time: 120 us -> 94.3 us (0.79)
  Pallas kernels: 114 us -> 87.8 us
  local copies, waits for them, and re-layouts: 0 us -> 3.16 us
  other arithmetic: 3.83 us -> 1.87 us
    pallas_call x3 -> x1, Pallas kernels: 114 us -> 87.8 us  [run_step(): pl.pallas_call(functools.partial(step_kernel, dims), out_shape=(jax.Shape...]
    unnamed x0 -> x1, local copies, waits for them, and re-layouts: none -> 3.16 us
    convert_element_type x1 -> x0, other arithmetic: 1.96 us -> none  [local(): blended = ((1.0 - t_value) ** 2 * point_start.astype(jnp.float32) + 2.0 *...]
where the time goes in v1:
time: 94.3 us; the launch traced here: 94.1 us
  Pallas kernels  87.8 us (93%)
  local copies, waits for them, and re-layouts  3.16 us (3%)
  other arithmetic  1.87 us (2%)
  between operations  1.29 us (1%)
    pallas_call x1, Pallas kernels, run_step(): pl.pallas_call(functools.partial(step_kernel, dims), out_shape=(jax.Shape...  87.8 us
    unnamed x1, local copies, waits for them, and re-layouts  3.16 us

profile of v1, /device:TPU:0, one launch (start us, length us, event | category | flops | bytes accessed | tf_op | source)
XLA Modules:
  0.0 94.1 jit_solution(3244080794284122993)
XLA Ops:
  1.3 87.8 %bezier_step.1 = (bf16[512,2048]{1,0:T(8,128)(2,1)}, f32[512,256]{1,0:T(8,128)}) custom-call(f32[1]{0:T(128)S(6)} %copy.10.t_ref, bf16[512,256]{1,0:T(8,128)(2,1)} %start_ref.1, bf16[512,256]{1,0:T(8,128)(2,1)} %mid_ref.1, bf16[512,256]{1,0:T(8,128)(2,1)} %end_ref.1, bf16[512,4096]{1,0:T(8,128)(2,1)} %hidden_ref.1, bf16[512,2048]{1,0:T(8,128)(2,1)} %query_ref.1, ...), custom_call_target="tpu_custom_call" | custom-call | tf_op jit(solution)/shard_map/bezier_step/pallas_call | solution.py:549
  89.0 1.9 %broadcast_multiply_fusion = f32[512,256]{1,0:T(8,128)} fusion(f32[512,256]{1,0:T(8,128)} %get-tuple-element.5, f32[]{:T(128)} %bitcast), kind=kLoop, calls=%fused_computation | loop fusion | flops 131072 | bytes 1048580 | tf_op jit(solution)/shard_map/mul | solution.py:567
  90.9 3.2 %copy.11 = bf16[512,2048]{1,0:T(8,128)(2,1)} copy(bf16[512,2048]{1,0:T(8,128)(2,1)} %get-tuple-element.8) | data formatting | bytes 4194304

commit v2 on v1

v2 whole, which is shorter than its diff:
```python
import functools
import math

import jax
import jax.numpy as jnp
from jax import lax
from jax.experimental import pallas as pl
from jax.experimental.pallas import tpu as pltpu
from jax.sharding import PartitionSpec as P

HD = 128
BQ = 256
MESH = pl.DeviceIdType.MESH
VMEM_LIMIT = 60 * 1024 * 1024


def rope_tables(seq_len, head_dim):
    shape = (seq_len, head_dim)
    positions = lax.broadcasted_iota(jnp.int32, shape, 0).astype(jnp.float32)
    column = lax.broadcasted_iota(jnp.int32, shape, 1)
    halves_index = jnp.where(column < head_dim // 2, column, column - head_dim // 2).astype(jnp.float32)
    inverse = jnp.exp(-(2.0 * halves_index / head_dim) * math.log(500000.0))
    angles = positions * inverse
    cosine, sine_t = jnp.cos(angles), jnp.sin(angles)
    return (cosine, sine_t)


def rotate(x):
    half = x.shape[-1] // 2
    return jnp.concatenate([-x[..., half:], x[..., :half]], axis=-1)


def rotate_back(x):
    half = x.shape[-1] // 2
    return jnp.concatenate([x[..., half:], -x[..., :half]], axis=-1)


NN = (((1,), (0,)), ((), ()))
NT = (((1,), (1,)), ((), ()))
TN = (((0,), (0,)), ((), ()))


def mm(x, y, dims=NN):
    return lax.dot_general(x, y, dims, preferred_element_type=jnp.float32)


ORDER = ((1, 0), (0, 1))


def place(dims):
    dp, fs = lax.axis_index("dp"), lax.axis_index("fsdp")
    return (dp // dims[1], dp % dims[1], fs // 2), fs % 2


def target(dims, at, core, axis=None, offset=0):
    at = list(at)
    if axis is not None:
        at[axis] = (at[axis] + offset + dims[axis]) % dims[axis]
    return (at[0] * dims[1] + at[1], at[2] * 2 + core)


def send(src, dst, send_sem, recv_sem, peer):
    return pltpu.make_async_remote_copy(
        src_ref=src, dst_ref=dst, send_sem=send_sem, recv_sem=recv_sem,
        device_id=peer, device_id_type=MESH)


def all_peers(dims, at, core):
    peers = [target(dims, at, core, axis, k) for axis in range(3) for k in range(1, dims[axis])]
    return peers + [target(dims, at, 1 - core)]


def attend_head(keys_at, values_at, q_cols, kv, q_ref, g_ref, cos_ref, sin_ref, ctx_ref, y_ref, kg, vg):
    seq = kv.shape[0]
    group = q_cols[1] // HD
    scale = 1.0 / math.sqrt(HD)
    to_base2 = scale * math.log2(math.e)

    def cols(g):
        return pl.ds(pl.multiple_of(q_cols[0] + g * HD, HD), HD)

    raw = kv[:, keys_at].astype(jnp.float32)
    cosine, sine_t = cos_ref[...], sin_ref[...]
    keys = (raw * cosine + rotate(raw) * sine_t).astype(jnp.bfloat16)
    values = kv[:, values_at]
    values_t = values.astype(jnp.float32).T.astype(jnp.bfloat16)
    kg[...] = jnp.zeros_like(kg)
    vg[...] = jnp.zeros_like(vg)
    for start in range(0, seq, BQ):
        nk = start + BQ
        rows = slice(start, nk)
        qs = jnp.concatenate([q_ref[rows, cols(g)] for g in range(group)], axis=0)
        gs = jnp.concatenate([g_ref[rows, cols(g)] for g in range(group)], axis=0)
        s = mm(keys[:nk], qs, NT)
        key_at = lax.broadcasted_iota(jnp.int32, (BQ, group * BQ), 0)
        query_at = lax.broadcasted_iota(jnp.int32, (BQ, group * BQ), 1) % BQ
        last = jnp.where(key_at <= query_at, s[start:], -1e30)
        s = last if start == 0 else jnp.concatenate([s[:start], last], axis=0)
        top = jnp.max(s, axis=0, keepdims=True)
        w = jnp.exp2((s - top) * to_base2)
        p = w * (1.0 / jnp.sum(w, axis=0, keepdims=True))
        p_low = p.astype(jnp.bfloat16)
        ctx_t = mm(values_t[:, :nk], p_low)
        dp = mm(values[:nk], gs, NT)
        vg[:nk] += mm(p_low, gs)
        delta = jnp.sum(dp * p, axis=0, keepdims=True)
        ds = (p * ((dp - delta) * scale)).astype(jnp.bfloat16)
        kg[:nk] += mm(ds, qs)
        ctx = ctx_t.T.astype(jnp.bfloat16)
        for g in range(group):
            ctx_ref[rows, cols(g)] = ctx[g * BQ:(g + 1) * BQ]
    rot = kg[...]
    y_ref[:, keys_at] = (rot * cosine + rotate_back(rot * sine_t)).astype(jnp.bfloat16)
    y_ref[:, values_at] = vg[...].astype(jnp.bfloat16)


def step_kernel(dims, t_ref, start_ref, mid_ref, end_ref, hidden_ref, query_ref, cot_ref, out_ctx, out_grad,
                pts, grad, hid, x2, qv, gv, ctx, cos_ref, sin_ref, full, acc, kv, kg, vg, y1, y2, early,
                load_sem, x_send, x_recv, y_send, y_recv, z_send, s_send, t_send, c_send,
                z_recv, t_recv, c_recv, *more):
    s_recv = more[:2]
    halves = [more[2:14], more[14:26]]
    at, core = place(dims)
    depth = dims[2]
    across = dims[0] * dims[1]
    rows = start_ref.shape[0]
    half = rows // 2
    groups = full.shape[0]
    last = groups - 1
    heads = across // 2
    other = target(dims, at, 1 - core)
    here = at[:2]

    def take_bytes(ref, sem):
        send(ref, ref, c_send.at[0], sem, other).wait_recv()

    def sent_bytes(ref, sem):
        send(ref, ref, sem, c_recv.at[0, 0], other).wait_send()


    def piece(p, c, h, zz, pos):
        col = pl.multiple_of((pos[0] * dims[1] + pos[1]) * HD, HD)
        return full.at[p, c, zz, pl.ds(h * half, half), pl.ds(col, HD)]

    def moved(axis, k):
        pos = [at[0], at[1]]
        pos[axis] = (pos[axis] + k) % dims[axis]
        return pos

    def push(p, h, zz, pos, send_sem, recv_sem, peer):
        ref = piece(p, core, h, zz, pos)
        return send(ref, ref, send_sem, recv_sem, peer)

    def near(k, act):
        @pl.loop(0, 2)
        def _(side):
            zz = at[2] + (2 * side - 1) * k
            pl.when((zz >= 0) & (zz < depth))(lambda: act(zz, side))

    def to_z(p, h, zz, side):
        push(p, h, zz, here, z_send.at[p, side, zz], z_recv.at[p, h, zz],
             target(dims, at, core, 2, 1 - 2 * side)).start()

    def onward(side):
        return ((side == 0) & (at[2] < depth - 1)) | ((side == 1) & (at[2] > 0))

    def to_second(p, h, zz, k):
        push(p, h, zz, here, s_send.at[p], s_recv[h].at[p, zz, k - 1],
             target(dims, at, core, ORDER[1 - h][0], k)).start()

    def to_third(p, h, zz, pos, k):
        push(p, h, zz, pos, t_send.at[p], t_recv.at[p, h, zz],
             target(dims, at, core, ORDER[1 - h][1], k)).start()

    def to_core(p, h, zz, pos):
        push(p, h, zz, pos, c_send.at[p], c_recv.at[p, zz], other).start()

    def swap_x(zz):
        src = pl.multiple_of((2 * zz + 1 - core) * rows, rows)
        dst = pl.multiple_of(zz * rows, rows)
        return send(hidden_ref.at[:, pl.ds(src, rows)], x2.at[:, pl.ds(dst, rows)],
                    x_send.at[0], x_recv.at[0], other)

    def own_z(p):
        @pl.loop(0, 2)
        def _(side):
            @pl.when(onward(side))
            def _():
                for h in range(2):
                    to_z(p, h, at[2], side)

    def send_all(p, h, zz):
        for k in range(1, dims[ORDER[1 - h][0]]):
            to_second(p, h, zz, k)
        for k in range(1, dims[ORDER[1 - h][1]]):
            to_third(p, h, zz, here, k)
        to_core(p, h, zz, here)

    def take_z(p, zz, side, more=True):
        for h in range(2):
            take_bytes(piece(p, core, h, zz, here), z_recv.at[p, h, zz])
            pl.when(onward(side))(lambda: to_z(p, h, zz, side))
            if more:
                send_all(p, h, zz)

    def relay_second(p, zz):
        for h in range(2):
            d2, d3 = ORDER[1 - h]
            for k2 in range(1, dims[d2]):
                pos = moved(d2, k2)
                take_bytes(piece(p, core, h, zz, pos), s_recv[h].at[p, zz, dims[d2] - k2 - 1])
                for k in range(1, dims[d3]):
                    to_third(p, h, zz, pos, k)
                to_core(p, h, zz, pos)

    def product(p, c, zz, first=False):
        x = hid[:, pl.ds(pl.multiple_of((2 * zz + c) * rows, rows), rows)]
        got = mm(x, full[p, c, zz])
        if first:
            acc[...] = got
        else:
            acc[...] += got

    def third(p, zz, first=False):
        for h in range(2):
            d2, d3 = ORDER[1 - h]
            count = (dims[d3] - 1) * dims[d2]
            take_bytes(full.at[p, core, zz, pl.ds(0, half), pl.ds(0, count * HD)], t_recv.at[p, h, zz])
            for k3 in range(1, dims[d3]):
                for k2 in range(dims[d2]):
                    pos = moved(d3, k3)
                    pos[d2] = (at[d2] + k2) % dims[d2]
                    to_core(p, h, zz, pos)
        product(p, core, zz, first)

    def from_core(p, zz):
        take_bytes(full.at[p, 1 - core, zz], c_recv.at[p, zz])
        product(p, 1 - core, zz)

    def drain_gather():
        seconds = dims[0] + dims[1] - 2
        thirds = (2 * across - dims[0] - dims[1]) // 2
        for p in range(groups):
            @pl.loop(0, depth)
            def _(zz):
                ref = full.at[p, core, zz, :, pl.ds(0, HD)]
                pl.when((zz <= at[2]) & (at[2] < depth - 1))(lambda: sent_bytes(ref, z_send.at[p, 0, zz]))
                pl.when((zz >= at[2]) & (at[2] > 0))(lambda: sent_bytes(ref, z_send.at[p, 1, zz]))

            sent_bytes(full.at[p, core, :, pl.ds(0, half), pl.ds(0, seconds * HD)], s_send.at[p])
            sent_bytes(full.at[p, core, :, :, pl.ds(0, thirds * HD)], t_send.at[p])
            sent_bytes(full.at[p, core], c_send.at[p])


    def first_copies(p, zz, same):
        for h in range(2):
            d1, d2 = ORDER[h]
            part, r1, q1 = halves[h][0], halves[h][1], halves[h][6 + same]
            for k1 in range(1, dims[d1]):
                v1 = (at[d1] + k1) % dims[d1]
                for k2 in (0,) if same else range(1, dims[d2]):
                    v2 = (at[d2] + k2) % dims[d2]
                    send(part.at[p, zz, v1, v2], r1.at[p, k1 - 1, zz, v2], halves[h][5].at[p], q1.at[p, zz],
                         target(dims, at, core, d1, k1)).start()

    def take_first(p, h, zz, same):
        count = 1 if same else dims[ORDER[h][1]] - 1
        take_bytes(halves[h][1].at[p, :, zz, pl.ds(0, count)], halves[h][6 + same].at[p, zz])

    def swap_y(p):
        return send(y1.at[p], y2.at[p], y_send.at[p], y_recv.at[p], other)

    def partial_own(p):
        @pl.loop(0, depth)
        def _(zz):
            x = hid[:, pl.ds(pl.multiple_of((2 * zz + core) * rows, rows), rows)]
            early[zz] = mm(x, y1[p], TN)

    def turn(step):
        return (at[2] + step) % depth

    def partial_sum(p, zz):
        x = x2[:, pl.ds(pl.multiple_of(zz * rows, rows), rows)]
        r = (early[zz] + mm(x, y2[p], TN)).astype(jnp.bfloat16)
        for dp in range(across):
            where = (dp // dims[1], dp % dims[1])
            for h in range(2):
                d1, d2 = ORDER[h]
                halves[h][0][p, zz, where[d1], where[d2]] = (
                    r[h * half:(h + 1) * half, dp * HD:(dp + 1) * HD])

    def keep1(p, h, zz, v2):
        d1, d2 = ORDER[h]
        part, r1 = halves[h][0], halves[h][1]
        total = part[p, zz, at[d1], v2].astype(jnp.float32)
        for k1 in range(1, dims[d1]):
            total += r1[p, k1 - 1, zz, v2].astype(jnp.float32)
        return total

    def sum_second(p, zz):
        for h in range(2):
            d2 = ORDER[h][1]
            sum2, r2 = halves[h][2], halves[h][3]
            take_first(p, h, zz, 0)
            for k2 in range(1, dims[d2]):
                v2 = (at[d2] + k2) % dims[d2]
                sum2[p, k2 - 1, zz] = keep1(p, h, zz, v2).astype(jnp.bfloat16)
                send(sum2.at[p, k2 - 1, zz], r2.at[p, k2 - 1, zz], halves[h][8].at[p], halves[h][9].at[p, zz],
                     target(dims, at, core, d2, k2)).start()

    def keep2(p, h, zz):
        d2 = ORDER[h][1]
        take_first(p, h, zz, 1)
        total = keep1(p, h, zz, at[d2])
        take_bytes(halves[h][3].at[p, :, zz], halves[h][9].at[p, zz])
        for k2 in range(1, dims[d2]):
            total += halves[h][3][p, k2 - 1, zz].astype(jnp.float32)
        return total

    def sum_third(p, step):
        zz = turn(step)
        for h in range(2):
            d1, d2 = ORDER[h]
            part, r3 = halves[h][0], halves[h][4]
            part[p, zz, at[d1], at[d2]] = keep2(p, h, zz).astype(jnp.bfloat16)
            send(part.at[p, zz, at[d1], at[d2]], r3.at[p, step - 1], halves[h][10].at[p], halves[h][11].at[p],
                 target(dims, at, core, 2, step)).start()

    def store(p):
        return pltpu.make_async_copy(grad.at[p], out_grad.at[:, pl.ds(p * HD, HD)], load_sem.at[7 + p])

    def finish(p):
        for h in range(2):
            total = keep2(p, h, at[2])
            take_bytes(halves[h][4].at[p], halves[h][11].at[p])
            for k in range(1, depth):
                total += halves[h][4][p, k - 1].astype(jnp.float32)
            grad[p, h * half:(h + 1) * half] = total
        store(p).start()

    def drain_reduce(p):
        for h in range(2):
            sent_bytes(halves[h][1].at[p], halves[h][5].at[p])
            sent_bytes(halves[h][3].at[p], halves[h][8].at[p])
            sent_bytes(halves[h][4].at[p], halves[h][10].at[p])


    points = [pltpu.make_async_copy(ref, pts.at[i], load_sem.at[i])
              for i, ref in enumerate((start_ref, mid_ref, end_ref))]
    wholes = [pltpu.make_async_copy(ref, dst, load_sem.at[3 + i])
              for i, (ref, dst) in enumerate(((hidden_ref, hid), (query_ref, qv), (cot_ref, gv)))]
    for load in points + wholes:
        load.start()
    barrier = pltpu.get_barrier_semaphore()
    peers = all_peers(dims, at, core)
    for peer in peers:
        pl.semaphore_signal(barrier, inc=1, device_id=peer, device_id_type=MESH)
    for load in points:
        load.wait()
    t_value = t_ref[0]
    blended = (
        (1.0 - t_value) * (1.0 - t_value) * pts[0].astype(jnp.float32)
        + 2.0 * t_value * (1.0 - t_value) * pts[1].astype(jnp.float32)
        + t_value * t_value * pts[2].astype(jnp.float32)
    ).astype(jnp.bfloat16)
    col = pl.multiple_of((at[0] * dims[1] + at[1]) * HD, HD)
    for p in range(groups):
        full[p, core, at[2], :, pl.ds(col, HD)] = blended[:, p * HD:(p + 1) * HD]
    pl.semaphore_wait(barrier, len(peers))

    def send_both(p, zz):
        for h in range(2):
            send_all(p, h, zz)

    own_z(0)
    for p in range(min(groups, 2)):
        send_both(p, at[2])

    @pl.loop(0, depth)
    def _(zz):
        swap_x(zz).start()

    cosine, sine_t = rope_tables(*cos_ref.shape)
    cos_ref[...] = cosine
    sin_ref[...] = sine_t

    def take_first_group(k):
        near(k, lambda zz, side: take_z(0, zz, side))

    def relay_first_group(k):
        near(k, lambda zz, side: relay_second(0, zz))

    take_first_group(1)
    relay_second(0, at[2])

    @pl.loop(2, depth)
    def _(k):
        take_first_group(k)
        if groups > 1:
            pl.when(k == depth - 2)(lambda: own_z(1))
        relay_first_group(k - 1)

    wholes[0].wait()
    if groups > 1:
        near(1, lambda zz, side: take_z(1, zz, side, False))
    third(0, at[2], True)
    relay_first_group(depth - 1)
    if groups > 1:
        near(1, lambda zz, side: send_both(1, zz))
    near(1, lambda zz, side: third(0, zz))
    from_core(0, at[2])

    @pl.loop(2, depth)
    def _(k):
        if groups > 1:
            pl.when(k < depth - 1)(lambda: near(k, lambda zz, side: take_z(1, zz, side)))
        near(k, lambda zz, side: third(0, zz))
        near(k - 1, lambda zz, side: from_core(0, zz))

    near(depth - 1, lambda zz, side: from_core(0, zz))
    if groups > 1:
        near(depth - 1, lambda zz, side: take_z(1, zz, side))
    wholes[1].wait()
    wholes[2].wait()

    def around(act):
        @pl.loop(0, depth)
        def _(i):
            act(turn(i))

    share = depth // heads
    early_steps = min(2, depth - 1)
    for p in range(groups):
        if p > 0:
            around(lambda zz: third(p, zz))
            around(lambda zz: from_core(p, zz))

            @pl.loop(1, early_steps + 1)
            def _(step):
                sum_second(p - 1, turn(step))

            @pl.loop(1, early_steps + 1)
            def _(step):
                first_copies(p - 1, turn(step), 1)
        kv[...] = acc[...].astype(jnp.bfloat16)
        if p < last:
            acc[...] = jnp.zeros_like(acc)

        @pl.loop(0, heads)
        def _(d):
            keys_at = pl.ds(pl.multiple_of(d * HD, HD), HD)
            values_at = pl.ds(pl.multiple_of((heads + d) * HD, HD), HD)
            width = qv.shape[1] // (heads * groups)
            attend_head(keys_at, values_at, ((d * groups + p) * width, width), kv, qv, gv, cos_ref,
                        sin_ref, ctx, y1.at[p], kg, vg)
            if p < last:
                @pl.loop(0, share)
                def _(i):
                    k = d * share + i
                    pl.when(k == 0)(lambda: relay_second(p + 1, at[2]))
                    pl.when(k > 0)(lambda: near(k, lambda zz, side: relay_second(p + 1, zz)))
            if p > 0:
                @pl.when(d == 0)
                def _():
                    @pl.loop(early_steps + 1, depth + 1)
                    def _(step):
                        sum_second(p - 1, turn(step))
                        first_copies(p - 1, turn(step), 1)

        swap_y(p).start()
        if p > 0:
            @pl.loop(1, early_steps + 1)
            def _(step):
                sum_third(p - 1, step)
        if p == last:
            context = pltpu.make_async_copy(ctx, out_ctx, load_sem.at[6])
            context.start()
        partial_own(p)
        if p == 0:
            take_bytes(x2, x_recv.at[0])
        swap_y(p).wait()
        if p < last:
            @pl.loop(1, depth + 1)
            def _(step):
                partial_sum(p, turn(step))
                first_copies(p, turn(step), 0)

    partial_sum(last, turn(1))
    first_copies(last, turn(1), 0)
    partial_sum(last, turn(2))
    first_copies(last, turn(2), 0)
    first_copies(last, turn(1), 1)

    @pl.loop(3, depth + 1)
    def _(step):
        partial_sum(last, turn(step))

    for p in range(last):
        @pl.loop(early_steps + 1, depth)
        def _(step):
            sum_third(p, step)

    sum_second(last, turn(1))
    first_copies(last, turn(2), 1)
    sum_second(last, turn(2))

    @pl.loop(3, depth)
    def _(step):
        first_copies(last, turn(step), 0)
        first_copies(last, turn(step), 1)

    first_copies(last, at[2], 0)
    for p in range(last):
        finish(p)
    drain_gather()
    sent_bytes(x2, x_send.at[0])

    @pl.loop(1, depth - 1)
    def _(step):
        sum_third(last, step)

    @pl.loop(3, depth)
    def _(step):
        sum_second(last, turn(step))

    first_copies(last, at[2], 1)
    sum_second(last, at[2])
    sum_third(last, depth - 1)
    for p in range(last):
        drain_reduce(p)
    finish(last)
    drain_reduce(last)
    context.wait()
    for p in range(groups):
        store(p).wait()


def run_step(dims, hidden, queries, cotangent, point_start, point_mid, point_end, curve_time):
    rows, cols = point_mid.shape
    seq = hidden.shape[0]
    a, b, z = dims
    groups = cols // HD
    half = rows // 2
    width = a * b * HD
    sem = pltpu.SemaphoreType.DMA

    def vm(*shape, dtype=jnp.bfloat16):
        return pltpu.VMEM(shape, dtype)

    f32 = jnp.float32
    scratch = [
        vm(3, rows, cols), vm(groups, rows, HD, dtype=f32), vm(*hidden.shape), vm(seq, z * rows),
        vm(*queries.shape), vm(*cotangent.shape),
        vm(*queries.shape), vm(seq, HD, dtype=f32), vm(seq, HD, dtype=f32),
        vm(groups, 2, z, rows, width), vm(seq, width, dtype=f32), vm(seq, width),
        vm(seq, HD, dtype=f32), vm(seq, HD, dtype=f32),
        vm(groups, seq, width), vm(groups, seq, width), vm(z, rows, width, dtype=f32),
        sem((7 + groups,)), sem((1,)), sem((1,)), sem((groups,)), sem((groups,)),
        sem((groups, 2, z)), sem((groups,)), sem((groups,)), sem((groups,)),
        sem((groups, 2, z)), sem((groups, 2, z)), sem((groups, z)),
    ]
    scratch += [sem((groups, z, dims[ORDER[1 - h][0]] - 1)) for h in range(2)]
    for h in range(2):
        n1, n2 = dims[ORDER[h][0]], dims[ORDER[h][1]]
        scratch += [
            vm(groups, z, n1, n2, half, HD), vm(groups, n1 - 1, z, n2, half, HD),
            vm(groups, n2 - 1, z, half, HD), vm(groups, n2 - 1, z, half, HD),
            vm(groups, z - 1, half, HD),
            sem((groups,)), sem((groups, z)), sem((groups, z)),
            sem((groups,)), sem((groups, z)),
            sem((groups,)), sem((groups,)),
        ]
    hbm = pl.BlockSpec(memory_space=pl.ANY)
    return pl.pallas_call(
        functools.partial(step_kernel, dims),
        out_shape=(
            jax.ShapeDtypeStruct(queries.shape, jnp.bfloat16),
            jax.ShapeDtypeStruct((rows, cols), f32),
        ),
        in_specs=[pl.BlockSpec(memory_space=pltpu.SMEM)] + [hbm] * 6,
        out_specs=(hbm, hbm),
        scratch_shapes=scratch,
        compiler_params=pltpu.CompilerParams(
            collective_id=1, has_side_effects=True, vmem_limit_bytes=VMEM_LIMIT),
        name="bezier_step",
    )(curve_time, point_start, point_mid, point_end, hidden, queries, cotangent)


def local(dims, hidden, queries, cotangent, point_start, point_mid, point_end, curve_time):
    t_value = curve_time[0]
    context, gradient = run_step(dims, hidden, queries, cotangent, point_start, point_mid, point_end, curve_time)
    return (context, gradient * (2.0 * t_value * (1.0 - t_value)))


def solution(mesh):
    dp, fsdp = mesh.shape["dp"], mesh.shape["fsdp"]
    dims = (dp // 2, 2, fsdp // 2)
    return jax.shard_map(
        functools.partial(local, dims),
        mesh=mesh,
        in_specs=(
            P(("dp", "fsdp"), None),
            P(("dp", "fsdp"), None),
            P(("dp", "fsdp"), None),
            P("fsdp", "dp"),
            P("fsdp", "dp"),
            P("fsdp", "dp"),
            P(),
        ),
        out_specs=(P(("dp", "fsdp"), None), P("fsdp", "dp")),
        check_vma=False,
    )
```

time: 94.3 us -> 87.6 us (0.929)
  Pallas kernels: 87.8 us -> 81.1 us
    pallas_call x1, Pallas kernels: 87.8 us -> 81.1 us  [run_step(): pl.pallas_call(functools.partial(step_kernel, dims), out_shape=(jax.Shape...]
where the time goes in v2:
time: 87.6 us; the launch traced here: 87.4 us
  Pallas kernels  81.1 us (93%)
  local copies, waits for them, and re-layouts  3.16 us (4%)
  other arithmetic  1.87 us (2%)
  between operations  1.29 us (1%)
    pallas_call x1, Pallas kernels, run_step(): pl.pallas_call(functools.partial(step_kernel, dims), out_shape=(jax.Shape...  81.1 us
    unnamed x1, local copies, waits for them, and re-layouts  3.16 us
    mul x1, other arithmetic, local(): return (context, gradient * (2.0 * t_value * (1.0 - t_value)))  1.87 us

profile of v2, /device:TPU:0, one launch (start us, length us, event | category | flops | bytes accessed | tf_op | source)
XLA Modules:
  0.0 87.4 jit_solution(5310706325622645181)
XLA Ops:
  1.3 81.1 %bezier_step.1 = (bf16[512,2048]{1,0:T(8,128)(2,1)}, f32[512,256]{1,0:T(8,128)}) custom-call(f32[1]{0:T(128)S(6)} %copy.10.t_ref, bf16[512,256]{1,0:T(8,128)(2,1)} %start_ref.1, bf16[512,256]{1,0:T(8,128)(2,1)} %mid_ref.1, bf16[512,256]{1,0:T(8,128)(2,1)} %end_ref.1, bf16[512,4096]{1,0:T(8,128)(2,1)} %hidden_ref.1, bf16[512,2048]{1,0:T(8,128)(2,1)} %query_ref.1, ...), custom_call_target="tpu_custom_call" | custom-call | tf_op jit(solution)/shard_map/bezier_step/pallas_call | solution.py:574
  82.4 1.9 %broadcast_multiply_fusion = f32[512,256]{1,0:T(8,128)} fusion(f32[512,256]{1,0:T(8,128)} %get-tuple-element.5, f32[]{:T(128)} %bitcast), kind=kLoop, calls=%fused_computation | loop fusion | flops 131072 | bytes 1048580 | tf_op jit(solution)/shard_map/mul | solution.py:592
  84.2 3.2 %copy.11 = bf16[512,2048]{1,0:T(8,128)(2,1)} copy(bf16[512,2048]{1,0:T(8,128)(2,1)} %get-tuple-element.8) | data formatting | bytes 4194304

commit v3 on v2

--- a/solution.py
+++ b/solution.py
@@ -114,8 +114,8 @@
     y_ref[:, values_at] = vg[...].astype(jnp.bfloat16)
 
 
-def step_kernel(dims, t_ref, start_ref, mid_ref, end_ref, hidden_ref, query_ref, cot_ref, out_ctx, out_grad,
-                pts, grad, hid, x2, qv, gv, ctx, cos_ref, sin_ref, full, acc, kv, kg, vg, y1, y2, early,
+def step_kernel(dims, t_ref, start_ref, mid_ref, end_ref, hidden_ref, query_ref, cot_ref, ctx, grad,
+                pts, hid, x2, qv, gv, cos_ref, sin_ref, full, acc, kv, kg, vg, y1, y2, early,
                 load_sem, x_send, x_recv, y_send, y_recv, z_send, s_send, t_send, c_send,
                 z_recv, t_recv, c_recv, *more):
     s_recv = more[:2]
@@ -326,17 +326,13 @@
             send(part.at[p, zz, at[d1], at[d2]], r3.at[p, step - 1], halves[h][10].at[p], halves[h][11].at[p],
                  target(dims, at, core, 2, step)).start()
 
-    def store(p):
-        return pltpu.make_async_copy(grad.at[p], out_grad.at[:, pl.ds(p * HD, HD)], load_sem.at[7 + p])
-
     def finish(p):
         for h in range(2):
             total = keep2(p, h, at[2])
             take_bytes(halves[h][4].at[p], halves[h][11].at[p])
             for k in range(1, depth):
                 total += halves[h][4][p, k - 1].astype(jnp.float32)
-            grad[p, h * half:(h + 1) * half] = total
-        store(p).start()
+            grad[h * half:(h + 1) * half, p * HD:(p + 1) * HD] = total
 
     def drain_reduce(p):
         for h in range(2):
@@ -472,9 +468,6 @@
             @pl.loop(1, early_steps + 1)
             def _(step):
                 sum_third(p - 1, step)
-        if p == last:
-            context = pltpu.make_async_copy(ctx, out_ctx, load_sem.at[6])
-            context.start()
         partial_own(p)
         if p == 0:
             take_bytes(x2, x_recv.at[0])
@@ -530,9 +523,6 @@
         drain_reduce(p)
     finish(last)
     drain_reduce(last)
-    context.wait()
-    for p in range(groups):
-        store(p).wait()
 
 
 def run_step(dims, hidden, queries, cotangent, point_start, point_mid, point_end, curve_time):
@@ -549,13 +539,13 @@
 
     f32 = jnp.float32
     scratch = [
-        vm(3, rows, cols), vm(groups, rows, HD, dtype=f32), vm(*hidden.shape), vm(seq, z * rows),
+        vm(3, rows, cols), vm(*hidden.shape), vm(seq, z * rows),
         vm(*queries.shape), vm(*cotangent.shape),
-        vm(*queries.shape), vm(seq, HD, dtype=f32), vm(seq, HD, dtype=f32),
+        vm(seq, HD, dtype=f32), vm(seq, HD, dtype=f32),
         vm(groups, 2, z, rows, width), vm(seq, width, dtype=f32), vm(seq, width),
         vm(seq, HD, dtype=f32), vm(seq, HD, dtype=f32),
         vm(groups, seq, width), vm(groups, seq, width), vm(z, rows, width, dtype=f32),
-        sem((7 + groups,)), sem((1,)), sem((1,)), sem((groups,)), sem((groups,)),
+        sem((6,)), sem((1,)), sem((1,)), sem((groups,)), sem((groups,)),
         sem((groups, 2, z)), sem((groups,)), sem((groups,)), sem((groups,)),
         sem((groups, 2, z)), sem((groups, 2, z)), sem((groups, z)),
     ]
@@ -574,11 +564,11 @@
     return pl.pallas_call(
         functools.partial(step_kernel, dims),
         out_shape=(
-            jax.ShapeDtypeStruct(queries.shape, jnp.bfloat16),
-            jax.ShapeDtypeStruct((rows, cols), f32),
+            pltpu.VMEM(queries.shape, jnp.bfloat16),
+            pltpu.VMEM((rows, cols), f32),
         ),
         in_specs=[pl.BlockSpec(memory_space=pltpu.SMEM)] + [hbm] * 6,
-        out_specs=(hbm, hbm),
+        out_specs=(pl.BlockSpec(memory_space=pltpu.VMEM),) * 2,
         scratch_shapes=scratch,
         compiler_params=pltpu.CompilerParams(
             collective_id=1, has_side_effects=True, vmem_limit_bytes=VMEM_LIMIT),

time: 87.6 us -> 83.9 us (0.958)
  local copies, waits for them, and re-layouts: 3.16 us -> 1.32 us
  other arithmetic: 1.87 us -> 0.83 us
    unnamed x1, local copies, waits for them, and re-layouts: 3.16 us -> 1.32 us
    mul x1, other arithmetic: 1.87 us -> 0.83 us  [local(): return (context, gradient * (2.0 * t_value * (1.0 - t_value)))]
where the time goes in v3:
time: 83.9 us; the launch traced here: 83.7 us
  Pallas kernels  80.3 us (96%)
  local copies, waits for them, and re-layouts  1.32 us (2%)
  between operations  1.29 us (2%)
    pallas_call x1, Pallas kernels, run_step(): pl.pallas_call(functools.partial(step_kernel, dims), out_shape=(pltpu.VME...  80.3 us

profile of v3, /device:TPU:0, one launch (start us, length us, event | category | flops | bytes accessed | tf_op | source)
XLA Modules:
  0.0 83.7 jit_solution(14035566393736480484)
XLA Ops:
  1.3 80.3 %bezier_step.1 = (bf16[512,2048]{1,0:T(8,128)(2,1)S(1)}, f32[512,256]{1,0:T(8,128)S(1)}) custom-call(f32[1]{0:T(128)S(6)} %copy.11.t_ref, bf16[512,256]{1,0:T(8,128)(2,1)} %start_ref.1, bf16[512,256]{1,0:T(8,128)(2,1)} %mid_ref.1, bf16[512,256]{1,0:T(8,128)(2,1)} %end_ref.1, bf16[512,4096]{1,0:T(8,128)(2,1)} %hidden_ref.1, bf16[512,2048]{1,0:T(8,128)(2,1)} %query_ref.1, ...), custom_call_target="tpu_custom_call" | custom-call | tf_op jit(solution)/shard_map/bezier_step/pallas_call | solution.py:564
  81.6 0.8 broadcast_multiply_fusion
  82.4 1.3 %copy.10 = bf16[512,2048]{1,0:T(8,128)(2,1)} copy(bf16[512,2048]{1,0:T(8,128)(2,1)S(1)} %get-tuple-element.6) | data formatting | bytes 4194304

commit v4 on v3

--- a/solution.py
+++ b/solution.py
@@ -267,14 +267,12 @@
         count = 1 if same else dims[ORDER[h][1]] - 1
         take_bytes(halves[h][1].at[p, :, zz, pl.ds(0, count)], halves[h][6 + same].at[p, zz])
 
-    def swap_y(p):
-        return send(y1.at[p], y2.at[p], y_send.at[p], y_recv.at[p], other)
-
-    def partial_own(p):
-        @pl.loop(0, depth)
-        def _(zz):
-            x = hid[:, pl.ds(pl.multiple_of((2 * zz + core) * rows, rows), rows)]
-            early[zz] = mm(x, y1[p], TN)
+    def swap_y(p, columns):
+        send(y1.at[p, :, columns], y2.at[p, :, columns], y_send.at[p], y_recv.at[p], other).start()
+
+    def partial_own(p, zz):
+        x = hid[:, pl.ds(pl.multiple_of((2 * zz + core) * rows, rows), rows)]
+        early[zz] = mm(x, y1[p], TN)
 
     def turn(step):
         return (at[2] + step) % depth
@@ -449,6 +447,8 @@
             width = qv.shape[1] // (heads * groups)
             attend_head(keys_at, values_at, ((d * groups + p) * width, width), kv, qv, gv, cos_ref,
                         sin_ref, ctx, y1.at[p], kg, vg)
+            swap_y(p, keys_at)
+            swap_y(p, values_at)
             if p < last:
                 @pl.loop(0, share)
                 def _(i):
@@ -463,18 +463,19 @@
                         sum_second(p - 1, turn(step))
                         first_copies(p - 1, turn(step), 1)
 
-        swap_y(p).start()
         if p > 0:
             @pl.loop(1, early_steps + 1)
             def _(step):
                 sum_third(p - 1, step)
-        partial_own(p)
+        partial_own(p, turn(1))
+        partial_own(p, turn(2))
         if p == 0:
             take_bytes(x2, x_recv.at[0])
-        swap_y(p).wait()
+        take_bytes(y2.at[p], y_recv.at[p])
         if p < last:
             @pl.loop(1, depth + 1)
             def _(step):
+                pl.when(step > 2)(lambda: partial_own(p, turn(step)))
                 partial_sum(p, turn(step))
                 first_copies(p, turn(step), 0)
 
@@ -486,6 +487,7 @@
 
     @pl.loop(3, depth + 1)
     def _(step):
+        partial_own(last, turn(step))
         partial_sum(last, turn(step))
 
     for p in range(last):
@@ -503,8 +505,6 @@
         first_copies(last, turn(step), 1)
 
     first_copies(last, at[2], 0)
-    for p in range(last):
-        finish(p)
     drain_gather()
     sent_bytes(x2, x_send.at[0])
 
@@ -519,7 +519,10 @@
     first_copies(last, at[2], 1)
     sum_second(last, at[2])
     sum_third(last, depth - 1)
+    for p in range(groups):
+        sent_bytes(y1.at[p], y_send.at[p])
     for p in range(last):
+        finish(p)
         drain_reduce(p)
     finish(last)
     drain_reduce(last)
@@ -576,10 +579,36 @@
     )(curve_time, point_start, point_mid, point_end, hidden, queries, cotangent)
 
 
+def close_kernel(t_ref, ctx_ref, grad_ref, out_ctx, out_grad, scaled, sems):
+    context = pltpu.make_async_copy(ctx_ref, out_ctx, sems.at[0])
+    context.start()
+    t_value = t_ref[0]
+    scaled[...] = grad_ref[...] * (2.0 * t_value * (1.0 - t_value))
+    gradient = pltpu.make_async_copy(scaled, out_grad, sems.at[1])
+    gradient.start()
+    context.wait()
+    gradient.wait()
+
+
+def close_step(curve_time, context, gradient):
+    hbm = pl.BlockSpec(memory_space=pl.ANY)
+    return pl.pallas_call(
+        close_kernel,
+        out_shape=(
+            jax.ShapeDtypeStruct(context.shape, context.dtype),
+            jax.ShapeDtypeStruct(gradient.shape, gradient.dtype),
+        ),
+        in_specs=[pl.BlockSpec(memory_space=pltpu.SMEM), hbm, pl.BlockSpec(memory_space=pltpu.VMEM)],
+        out_specs=(hbm, hbm),
+        scratch_shapes=[pltpu.VMEM(gradient.shape, gradient.dtype), pltpu.SemaphoreType.DMA((2,))],
+        compiler_params=pltpu.CompilerParams(vmem_limit_bytes=8 * 1024 * 1024),
+        name="close_step",
+    )(curve_time, context, gradient)
+
+
 def local(dims, hidden, queries, cotangent, point_start, point_mid, point_end, curve_time):
-    t_value = curve_time[0]
-    context, gradient = run_step(dims, hidden, queries, cotangent, point_start, point_mid, point_end, curve_time)
-    return (context, gradient * (2.0 * t_value * (1.0 - t_value)))
+    return close_step(curve_time, *run_step(
+        dims, hidden, queries, cotangent, point_start, point_mid, point_end, curve_time))
 
 
 def solution(mesh):

time: 83.9 us -> 82.9 us (0.988)
  local copies, waits for them, and re-layouts: 1.32 us -> 0 us
  Pallas kernels: 80.3 us -> 81.3 us
    pallas_call x0 -> x1, Pallas kernels: none -> 1.5 us  [close_step(): pl.pallas_call(close_kernel, out_shape=(jax.ShapeDtypeStruct(context.shap...]
    unnamed x1 -> x0, local copies, waits for them, and re-layouts: 1.32 us -> none
where the time goes in v4:
time: 82.9 us; the launch traced here: 82.8 us
  Pallas kernels  81.3 us (98%)
  between operations  1.45 us (2%)
    pallas_call x1, Pallas kernels, run_step(): pl.pallas_call(functools.partial(step_kernel, dims), out_shape=(pltpu.VME...  79.8 us

profile of v4, /device:TPU:0, one launch (start us, length us, event | category | flops | bytes accessed | tf_op | source)
XLA Modules:
  0.0 82.8 jit_solution(12605055510493221113)
XLA Ops:
  1.3 79.8 %bezier_step.1 = (bf16[512,2048]{1,0:T(8,128)(2,1)S(1)}, f32[512,256]{1,0:T(8,128)S(1)}) custom-call(f32[1]{0:T(128)S(6)} %copy.9.t_ref, bf16[512,256]{1,0:T(8,128)(2,1)} %start_ref.1, bf16[512,256]{1,0:T(8,128)(2,1)} %mid_ref.1, bf16[512,256]{1,0:T(8,128)(2,1)} %end_ref.1, bf16[512,4096]{1,0:T(8,128)(2,1)} %hidden_ref.1, bf16[512,2048]{1,0:T(8,128)(2,1)} %query_ref.1, ...), custom_call_target="tpu_custom_call" | custom-call | tf_op jit(solution)/shard_map/bezier_step/pallas_call | solution.py:567
  81.1 1.5 %close_step.1 = (bf16[512,2048]{1,0:T(8,128)(2,1)}, f32[512,256]{1,0:T(8,128)}) custom-call(f32[1]{0:T(128)S(6)} %copy.9.t_ref, bf16[512,2048]{1,0:T(8,128)(2,1)S(1)} %get-tuple-element.4.ctx_ref, f32[512,256]{1,0:T(8,128)S(1)} %get-tuple-element.5.grad_ref), custom_call_target="tpu_custom_call" | custom-call | tf_op jit(solution)/shard_map/close_step/pallas_call | solution.py:595

commit v5 on v4

--- a/solution.py
+++ b/solution.py
@@ -117,9 +117,9 @@
 def step_kernel(dims, t_ref, start_ref, mid_ref, end_ref, hidden_ref, query_ref, cot_ref, ctx, grad,
                 pts, hid, x2, qv, gv, cos_ref, sin_ref, full, acc, kv, kg, vg, y1, y2, early,
                 load_sem, x_send, x_recv, y_send, y_recv, z_send, s_send, t_send, c_send,
-                z_recv, t_recv, c_recv, *more):
+                z_recv, t_recv, c_recv, same_recv, rest_recv, second_recv, *more):
     s_recv = more[:2]
-    halves = [more[2:14], more[14:26]]
+    halves = [more[2:11], more[11:20]]
     at, core = place(dims)
     depth = dims[2]
     across = dims[0] * dims[1]
@@ -252,20 +252,27 @@
             sent_bytes(full.at[p, core], c_send.at[p])
 
 
-    def first_copies(p, zz, same):
+    def cut(p):
+        return 2 if p == last else 1
+
+    def sub(p, r):
+        size = half // cut(p)
+        return pl.ds(pl.multiple_of(r * size, size), size)
+
+    def take_pieces(p, count, sem):
+        take_bytes(full.at[0, core, 0, pl.ds(0, half // cut(p)), pl.ds(0, count * HD)], sem)
+
+    def first_copies(p, zz, r, same):
         for h in range(2):
             d1, d2 = ORDER[h]
-            part, r1, q1 = halves[h][0], halves[h][1], halves[h][6 + same]
+            part, r1 = halves[h][0], halves[h][1]
+            sem = (same_recv if same else rest_recv).at[p, zz, r]
             for k1 in range(1, dims[d1]):
                 v1 = (at[d1] + k1) % dims[d1]
                 for k2 in (0,) if same else range(1, dims[d2]):
                     v2 = (at[d2] + k2) % dims[d2]
-                    send(part.at[p, zz, v1, v2], r1.at[p, k1 - 1, zz, v2], halves[h][5].at[p], q1.at[p, zz],
-                         target(dims, at, core, d1, k1)).start()
-
-    def take_first(p, h, zz, same):
-        count = 1 if same else dims[ORDER[h][1]] - 1
-        take_bytes(halves[h][1].at[p, :, zz, pl.ds(0, count)], halves[h][6 + same].at[p, zz])
+                    send(part.at[p, zz, v1, v2, sub(p, r)], r1.at[p, k1 - 1, zz, v2, sub(p, r)],
+                         halves[h][5].at[p], sem, target(dims, at, core, d1, k1)).start()
 
     def swap_y(p, columns):
         send(y1.at[p, :, columns], y2.at[p, :, columns], y_send.at[p], y_recv.at[p], other).start()
@@ -287,56 +294,62 @@
                 halves[h][0][p, zz, where[d1], where[d2]] = (
                     r[h * half:(h + 1) * half, dp * HD:(dp + 1) * HD])
 
-    def keep1(p, h, zz, v2):
+    def keep1(p, h, zz, v2, r):
         d1, d2 = ORDER[h]
         part, r1 = halves[h][0], halves[h][1]
-        total = part[p, zz, at[d1], v2].astype(jnp.float32)
+        total = part[p, zz, at[d1], v2, sub(p, r)].astype(jnp.float32)
         for k1 in range(1, dims[d1]):
-            total += r1[p, k1 - 1, zz, v2].astype(jnp.float32)
+            total += r1[p, k1 - 1, zz, v2, sub(p, r)].astype(jnp.float32)
         return total
 
-    def sum_second(p, zz):
+    def sum_second(p, zz, r):
+        take_pieces(p, 2 * (dims[0] - 1) * (dims[1] - 1), rest_recv.at[p, zz, r])
         for h in range(2):
             d2 = ORDER[h][1]
             sum2, r2 = halves[h][2], halves[h][3]
-            take_first(p, h, zz, 0)
             for k2 in range(1, dims[d2]):
                 v2 = (at[d2] + k2) % dims[d2]
-                sum2[p, k2 - 1, zz] = keep1(p, h, zz, v2).astype(jnp.bfloat16)
-                send(sum2.at[p, k2 - 1, zz], r2.at[p, k2 - 1, zz], halves[h][8].at[p], halves[h][9].at[p, zz],
-                     target(dims, at, core, d2, k2)).start()
-
-    def keep2(p, h, zz):
-        d2 = ORDER[h][1]
-        take_first(p, h, zz, 1)
-        total = keep1(p, h, zz, at[d2])
-        take_bytes(halves[h][3].at[p, :, zz], halves[h][9].at[p, zz])
-        for k2 in range(1, dims[d2]):
-            total += halves[h][3][p, k2 - 1, zz].astype(jnp.float32)
+                sum2[p, k2 - 1, zz, sub(p, r)] = keep1(p, h, zz, v2, r).astype(jnp.bfloat16)
+                send(sum2.at[p, k2 - 1, zz, sub(p, r)], r2.at[p, k2 - 1, zz, sub(p, r)], halves[h][6].at[p],
+                     second_recv.at[p, zz, r], target(dims, at, core, d2, k2)).start()
+
+    def take_second(p, zz, r):
+        take_pieces(p, dims[0] + dims[1] - 2, same_recv.at[p, zz, r])
+        take_pieces(p, dims[0] + dims[1] - 2, second_recv.at[p, zz, r])
+
+    def keep2(p, h, zz, r):
+        total = keep1(p, h, zz, at[ORDER[h][1]], r)
+        for k2 in range(1, dims[ORDER[h][1]]):
+            total += halves[h][3][p, k2 - 1, zz, sub(p, r)].astype(jnp.float32)
         return total
 
-    def sum_third(p, step):
+    def sum_third(p, step, r):
         zz = turn(step)
+        take_second(p, zz, r)
         for h in range(2):
             d1, d2 = ORDER[h]
             part, r3 = halves[h][0], halves[h][4]
-            part[p, zz, at[d1], at[d2]] = keep2(p, h, zz).astype(jnp.bfloat16)
-            send(part.at[p, zz, at[d1], at[d2]], r3.at[p, step - 1], halves[h][10].at[p], halves[h][11].at[p],
-                 target(dims, at, core, 2, step)).start()
+            part[p, zz, at[d1], at[d2], sub(p, r)] = keep2(p, h, zz, r).astype(jnp.bfloat16)
+            send(part.at[p, zz, at[d1], at[d2], sub(p, r)], r3.at[p, step - 1, sub(p, r)], halves[h][7].at[p],
+                 halves[h][8].at[p], target(dims, at, core, 2, step)).start()
 
     def finish(p):
-        for h in range(2):
-            total = keep2(p, h, at[2])
-            take_bytes(halves[h][4].at[p], halves[h][11].at[p])
-            for k in range(1, depth):
-                total += halves[h][4][p, k - 1].astype(jnp.float32)
-            grad[h * half:(h + 1) * half, p * HD:(p + 1) * HD] = total
+        size = half // cut(p)
+        for r in range(cut(p)):
+            take_second(p, at[2], r)
+        for h in range(2):
+            take_bytes(halves[h][4].at[p], halves[h][8].at[p])
+            for r in range(cut(p)):
+                total = keep2(p, h, at[2], r)
+                for k in range(1, depth):
+                    total += halves[h][4][p, k - 1, sub(p, r)].astype(jnp.float32)
+                grad[h * half + r * size:h * half + (r + 1) * size, p * HD:(p + 1) * HD] = total
 
     def drain_reduce(p):
         for h in range(2):
             sent_bytes(halves[h][1].at[p], halves[h][5].at[p])
-            sent_bytes(halves[h][3].at[p], halves[h][8].at[p])
-            sent_bytes(halves[h][4].at[p], halves[h][10].at[p])
+            sent_bytes(halves[h][3].at[p], halves[h][6].at[p])
+            sent_bytes(halves[h][4].at[p], halves[h][7].at[p])
 
 
     points = [pltpu.make_async_copy(ref, pts.at[i], load_sem.at[i])
@@ -431,11 +444,11 @@
 
             @pl.loop(1, early_steps + 1)
             def _(step):
-                sum_second(p - 1, turn(step))
+                sum_second(p - 1, turn(step), 0)
 
             @pl.loop(1, early_steps + 1)
             def _(step):
-                first_copies(p - 1, turn(step), 1)
+                first_copies(p - 1, turn(step), 0, 1)
         kv[...] = acc[...].astype(jnp.bfloat16)
         if p < last:
             acc[...] = jnp.zeros_like(acc)
@@ -460,13 +473,13 @@
                 def _():
                     @pl.loop(early_steps + 1, depth + 1)
                     def _(step):
-                        sum_second(p - 1, turn(step))
-                        first_copies(p - 1, turn(step), 1)
+                        sum_second(p - 1, turn(step), 0)
+                        first_copies(p - 1, turn(step), 0, 1)
 
         if p > 0:
             @pl.loop(1, early_steps + 1)
             def _(step):
-                sum_third(p - 1, step)
+                sum_third(p - 1, step, 0)
         partial_own(p, turn(1))
         partial_own(p, turn(2))
         if p == 0:
@@ -477,13 +490,27 @@
             def _(step):
                 pl.when(step > 2)(lambda: partial_own(p, turn(step)))
                 partial_sum(p, turn(step))
-                first_copies(p, turn(step), 0)
-
+                first_copies(p, turn(step), 0, 0)
+
+    def slot(n):
+        i = n // 2 + 1
+        return jnp.where(i == 1, 2, jnp.where(i == 2, 1, i)), n % 2
+
+    def first_of(n, same):
+        step, r = slot(n)
+        first_copies(last, turn(step), r, same)
+
+    def third_of(n):
+        step, r = slot(n)
+        sum_third(last, step, r)
+
+    items = 2 * depth
+    partial_sum(last, turn(2))
+    for same in range(2):
+        for n in range(2):
+            first_of(n, same)
     partial_sum(last, turn(1))
-    first_copies(last, turn(1), 0)
-    partial_sum(last, turn(2))
-    first_copies(last, turn(2), 0)
-    first_copies(last, turn(1), 1)
+    first_of(2, 0)
 
     @pl.loop(3, depth + 1)
     def _(step):
@@ -493,32 +520,30 @@
     for p in range(last):
         @pl.loop(early_steps + 1, depth)
         def _(step):
-            sum_third(p, step)
-
-    sum_second(last, turn(1))
-    first_copies(last, turn(2), 1)
-    sum_second(last, turn(2))
-
-    @pl.loop(3, depth)
-    def _(step):
-        first_copies(last, turn(step), 0)
-        first_copies(last, turn(step), 1)
-
-    first_copies(last, at[2], 0)
+            sum_third(p, step, 0)
+
+    own = items - 2
+
+    @pl.loop(0, own)
+    def _(n):
+        step, r = slot(n)
+        sum_second(last, turn(step), r)
+        pl.when(n + 2 < own)(lambda: first_of(n + 2, 1))
+        pl.when(n + 3 < own)(lambda: first_of(n + 3, 0))
+
+        for same in range(2):
+            @pl.when(n == own - 2 + same)
+            def _():
+                first_of(own, same)
+                first_of(own + 1, same)
+
+        pl.when(n > 0)(lambda: third_of(n - 1))
+
+    for n in (own, own + 1):
+        sum_second(last, at[2], n - own)
+    third_of(own - 1)
     drain_gather()
     sent_bytes(x2, x_send.at[0])
-
-    @pl.loop(1, depth - 1)
-    def _(step):
-        sum_third(last, step)
-
-    @pl.loop(3, depth)
-    def _(step):
-        sum_second(last, turn(step))
-
-    first_copies(last, at[2], 1)
-    sum_second(last, at[2])
-    sum_third(last, depth - 1)
     for p in range(groups):
         sent_bytes(y1.at[p], y_send.at[p])
     for p in range(last):
@@ -551,6 +576,7 @@
         sem((6,)), sem((1,)), sem((1,)), sem((groups,)), sem((groups,)),
         sem((groups, 2, z)), sem((groups,)), sem((groups,)), sem((groups,)),
         sem((groups, 2, z)), sem((groups, 2, z)), sem((groups, z)),
+        sem((groups, z, 2)), sem((groups, z, 2)), sem((groups, z, 2)),
     ]
     scratch += [sem((groups, z, dims[ORDER[1 - h][0]] - 1)) for h in range(2)]
     for h in range(2):
@@ -559,9 +585,7 @@
             vm(groups, z, n1, n2, half, HD), vm(groups, n1 - 1, z, n2, half, HD),
             vm(groups, n2 - 1, z, half, HD), vm(groups, n2 - 1, z, half, HD),
             vm(groups, z - 1, half, HD),
-            sem((groups,)), sem((groups, z)), sem((groups, z)),
-            sem((groups,)), sem((groups, z)),
-            sem((groups,)), sem((groups,)),
+            sem((groups,)), sem((groups,)), sem((groups,)), sem((groups,)),
         ]
     hbm = pl.BlockSpec(memory_space=pl.ANY)
     return pl.pallas_call(

time: 82.9 us -> 81.4 us (0.982)
  Pallas kernels: 81.3 us -> 79.8 us
    pallas_call x1, Pallas kernels: 79.8 us -> 78.3 us  [run_step(): pl.pallas_call(functools.partial(step_kernel, dims), out_shape=(pltpu.VME...]
where the time goes in v5:
time: 81.4 us; the launch traced here: 81.3 us
  Pallas kernels  79.8 us (98%)
  between operations  1.45 us (2%)
    pallas_call x1, Pallas kernels, run_step(): pl.pallas_call(functools.partial(step_kernel, dims), out_shape=(pltpu.VME...  78.3 us

profile of v5, /device:TPU:0, one launch (start us, length us, event | category | flops | bytes accessed | tf_op | source)
XLA Modules:
  0.0 81.3 jit_solution(8546148508065521982)
XLA Ops:
  1.3 78.3 %bezier_step.1 = (bf16[512,2048]{1,0:T(8,128)(2,1)S(1)}, f32[512,256]{1,0:T(8,128)S(1)}) custom-call(f32[1]{0:T(128)S(6)} %copy.9.t_ref, bf16[512,256]{1,0:T(8,128)(2,1)} %start_ref.1, bf16[512,256]{1,0:T(8,128)(2,1)} %mid_ref.1, bf16[512,256]{1,0:T(8,128)(2,1)} %end_ref.1, bf16[512,4096]{1,0:T(8,128)(2,1)} %hidden_ref.1, bf16[512,2048]{1,0:T(8,128)(2,1)} %query_ref.1, ...), custom_call_target="tpu_custom_call" | custom-call | tf_op jit(solution)/shard_map/bezier_step/pallas_call | solution.py:591
  79.6 1.5 %close_step.1 = (bf16[512,2048]{1,0:T(8,128)(2,1)}, f32[512,256]{1,0:T(8,128)}) custom-call(f32[1]{0:T(128)S(6)} %copy.9.t_ref, bf16[512,2048]{1,0:T(8,128)(2,1)S(1)} %get-tuple-element.4.ctx_ref, f32[512,256]{1,0:T(8,128)S(1)} %get-tuple-element.5.grad_ref), custom_call_target="tpu_custom_call" | custom-call | tf_op jit(solution)/shard_map/close_step/pallas_call | solution.py:619

commit v6 on v5

--- a/solution.py
+++ b/solution.py
@@ -158,7 +158,7 @@
             pl.when((zz >= 0) & (zz < depth))(lambda: act(zz, side))
 
     def to_z(p, h, zz, side):
-        push(p, h, zz, here, z_send.at[p, side, zz], z_recv.at[p, h, zz],
+        push(p, h, zz, here, z_send.at[p, zz + side], z_recv.at[p, h, zz],
              target(dims, at, core, 2, 1 - 2 * side)).start()
 
     def onward(side):
@@ -169,7 +169,7 @@
              target(dims, at, core, ORDER[1 - h][0], k)).start()
 
     def to_third(p, h, zz, pos, k):
-        push(p, h, zz, pos, t_send.at[p], t_recv.at[p, h, zz],
+        push(p, h, zz, pos, t_send.at[p], t_recv.at[p, zz],
              target(dims, at, core, ORDER[1 - h][1], k)).start()
 
     def to_core(p, h, zz, pos):
@@ -222,10 +222,10 @@
             acc[...] += got
 
     def third(p, zz, first=False):
+        count = (2 * across - dims[0] - dims[1]) // 2
+        take_bytes(full.at[p, core, zz, :, pl.ds(0, count * HD)], t_recv.at[p, zz])
         for h in range(2):
             d2, d3 = ORDER[1 - h]
-            count = (dims[d3] - 1) * dims[d2]
-            take_bytes(full.at[p, core, zz, pl.ds(0, half), pl.ds(0, count * HD)], t_recv.at[p, h, zz])
             for k3 in range(1, dims[d3]):
                 for k2 in range(dims[d2]):
                     pos = moved(d3, k3)
@@ -244,8 +244,8 @@
             @pl.loop(0, depth)
             def _(zz):
                 ref = full.at[p, core, zz, :, pl.ds(0, HD)]
-                pl.when((zz <= at[2]) & (at[2] < depth - 1))(lambda: sent_bytes(ref, z_send.at[p, 0, zz]))
-                pl.when((zz >= at[2]) & (at[2] > 0))(lambda: sent_bytes(ref, z_send.at[p, 1, zz]))
+                pl.when((zz <= at[2]) & (at[2] < depth - 1))(lambda: sent_bytes(ref, z_send.at[p, zz]))
+                pl.when((zz >= at[2]) & (at[2] > 0))(lambda: sent_bytes(ref, z_send.at[p, zz + 1]))
 
             sent_bytes(full.at[p, core, :, pl.ds(0, half), pl.ds(0, seconds * HD)], s_send.at[p])
             sent_bytes(full.at[p, core, :, :, pl.ds(0, thirds * HD)], t_send.at[p])
@@ -266,7 +266,7 @@
         for h in range(2):
             d1, d2 = ORDER[h]
             part, r1 = halves[h][0], halves[h][1]
-            sem = (same_recv if same else rest_recv).at[p, zz, r]
+            sem = (same_recv if same else rest_recv).at[zz, p + r]
             for k1 in range(1, dims[d1]):
                 v1 = (at[d1] + k1) % dims[d1]
                 for k2 in (0,) if same else range(1, dims[d2]):
@@ -303,7 +303,7 @@
         return total
 
     def sum_second(p, zz, r):
-        take_pieces(p, 2 * (dims[0] - 1) * (dims[1] - 1), rest_recv.at[p, zz, r])
+        take_pieces(p, 2 * (dims[0] - 1) * (dims[1] - 1), rest_recv.at[zz, p + r])
         for h in range(2):
             d2 = ORDER[h][1]
             sum2, r2 = halves[h][2], halves[h][3]
@@ -311,11 +311,11 @@
                 v2 = (at[d2] + k2) % dims[d2]
                 sum2[p, k2 - 1, zz, sub(p, r)] = keep1(p, h, zz, v2, r).astype(jnp.bfloat16)
                 send(sum2.at[p, k2 - 1, zz, sub(p, r)], r2.at[p, k2 - 1, zz, sub(p, r)], halves[h][6].at[p],
-                     second_recv.at[p, zz, r], target(dims, at, core, d2, k2)).start()
+                     second_recv.at[zz, p + r], target(dims, at, core, d2, k2)).start()
 
     def take_second(p, zz, r):
-        take_pieces(p, dims[0] + dims[1] - 2, same_recv.at[p, zz, r])
-        take_pieces(p, dims[0] + dims[1] - 2, second_recv.at[p, zz, r])
+        take_pieces(p, dims[0] + dims[1] - 2, same_recv.at[zz, p + r])
+        take_pieces(p, dims[0] + dims[1] - 2, second_recv.at[zz, p + r])
 
     def keep2(p, h, zz, r):
         total = keep1(p, h, zz, at[ORDER[h][1]], r)
@@ -574,9 +574,9 @@
         vm(seq, HD, dtype=f32), vm(seq, HD, dtype=f32),
         vm(groups, seq, width), vm(groups, seq, width), vm(z, rows, width, dtype=f32),
         sem((6,)), sem((1,)), sem((1,)), sem((groups,)), sem((groups,)),
-        sem((groups, 2, z)), sem((groups,)), sem((groups,)), sem((groups,)),
-        sem((groups, 2, z)), sem((groups, 2, z)), sem((groups, z)),
-        sem((groups, z, 2)), sem((groups, z, 2)), sem((groups, z, 2)),
+        sem((groups, z + 1)), sem((groups,)), sem((groups,)), sem((groups,)),
+        sem((groups, 2, z)), sem((groups, z)), sem((groups, z)),
+        sem((z, groups + 1)), sem((z, groups + 1)), sem((z, groups + 1)),
     ]
     scratch += [sem((groups, z, dims[ORDER[1 - h][0]] - 1)) for h in range(2)]
     for h in range(2):

time: 81.4 us -> 81.2 us (level)
  no operation moved by 1% of the time
where the time goes in v6:
time: 81.2 us; the launch traced here: 81 us
  Pallas kernels  79.6 us (98%)
  between operations  1.45 us (2%)
    pallas_call x1, Pallas kernels, run_step(): pl.pallas_call(functools.partial(step_kernel, dims), out_shape=(pltpu.VME...  78.1 us

profile of v6, /device:TPU:0, one launch (start us, length us, event | category | flops | bytes accessed | tf_op | source)
XLA Modules:
  0.0 81.0 jit_solution(5404940158420997307)
XLA Ops:
  1.3 78.1 %bezier_step.1 = (bf16[512,2048]{1,0:T(8,128)(2,1)S(1)}, f32[512,256]{1,0:T(8,128)S(1)}) custom-call(f32[1]{0:T(128)S(6)} %copy.9.t_ref, bf16[512,256]{1,0:T(8,128)(2,1)} %start_ref.1, bf16[512,256]{1,0:T(8,128)(2,1)} %mid_ref.1, bf16[512,256]{1,0:T(8,128)(2,1)} %end_ref.1, bf16[512,4096]{1,0:T(8,128)(2,1)} %hidden_ref.1, bf16[512,2048]{1,0:T(8,128)(2,1)} %query_ref.1, ...), custom_call_target="tpu_custom_call" | custom-call | tf_op jit(solution)/shard_map/bezier_step/pallas_call | solution.py:591
  79.3 1.5 %close_step.1 = (bf16[512,2048]{1,0:T(8,128)(2,1)}, f32[512,256]{1,0:T(8,128)}) custom-call(f32[1]{0:T(128)S(6)} %copy.9.t_ref, bf16[512,2048]{1,0:T(8,128)(2,1)S(1)} %get-tuple-element.4.ctx_ref, f32[512,256]{1,0:T(8,128)S(1)} %get-tuple-element.5.grad_ref), custom_call_target="tpu_custom_call" | custom-call | tf_op jit(solution)/shard_map/close_step/pallas_call | solution.py:619
